TPU v7x, 256 devices: a whole 4x4x8 slice. The times are simulated.
256 devices in a mesh: gx: 4 (over x), gy: 16 (over z_lo, y), gz: 4 (over z_hi, core).
Axes of the slice: x: 4, y: 4, z: 8 (z_hi: 2, z_lo: 4; z = z_hi * 4 + z_lo), core: 2. Of those that a mesh axis runs over, the one named last changes fastest.
Arguments:
- atom_embedding: bfloat16 [4, 16, 4, 64, 512], P('gx', 'gy', 'gz'), may hold values from -6 to 6
- output_adjoint: bfloat16 [4, 16, 4, 64, 512], P('gx', 'gy', 'gz'), may hold values from -6 to 6
- fractional_coords: float32 [4, 16, 4, 3, 512], P('gx', 'gy', 'gz'), may hold values from 0 to 1, as said below
- element_labels: int32 [4, 16, 4, 512], P('gx', 'gy', 'gz'), may hold values from 0 to 3
- adjacent_ghost_entries: int32 [4, 16, 4, 16, 512], P('gx', 'gy', 'gz'), may hold values from 0 to 13823, as said below
- miller_triples: int32 [3, 2048], replicated, may hold values from -8 to 8
- reciprocal_kernel: float32 [2048, 64], replicated, may hold values from 0.02 to 0.2
- channel_mixing_matrix: bfloat16 [64, 64], replicated, may hold values from -0.75 to 0.75
- element_channel_factor: float32 [4, 64], replicated, may hold values from 0.25 to 1.75
- distance_kernel: float32 [16, 64], replicated, may hold values from -1.5 to 1.5
Outputs:
- atom_grad: bfloat16 [4, 16, 4, 64, 512], P('gx', 'gy', 'gz')
- position_grad: float32 [4, 16, 4, 3, 512], P('gx', 'gy', 'gz')
- weight_grad: float32 [64, 64], replicated
- radial_grad: float32 [16, 64], replicated
- filter_grad: float32 [2048, 64], P(('gx', 'gy', 'gz'))
Inputs may be any that keep to these rules, and one draw needn't show every extreme that they name: `adjacent_ghost_entries`: the atoms of a brick form 32 blocks of 16 in order; block q < 27 is the cell of offset (q // 9 - 1, (q // 3) % 3 - 1, q % 3 - 1) of the brick, blocks 27 to 31 lie in its central cell. A ghost entry e names atom e % 512 of slot e // 512; an entry in a slot of offset o names an atom of a block whose cell offset equals -o in every dimension where o is not zero, and o is zero in every dimension where the listing atom's cell offset is zero; every slot occurs. `fractional_coords`: an atom of a block whose cell offset is -1 or 1 in a dimension lies within a quarter of the brick length of that face in that dimension. `miller_triples`: integer components; any triple may occur, the zero triple too.
All inputs are finite; a program needn't handle non-finite values.
Results may differ from a plain program's by a relative error of at most 0.0053.
Values may be sent and summed in bfloat16 or wider, within the bound.
A program may use at most 128 MiB of HBM per device.

v0:
```python
import functools
import math

import jax
import jax.numpy as jnp
from jax import lax
from jax.sharding import Mesh
from jax.sharding import PartitionSpec as P

GY = ("gy_0", "gy_1")
GZ = ("gz_0", "gz_1")
GX_GY_GZ = ("gx", "gy_0", "gy_1", "gz_0", "gz_1")


circle_angle = 2.0 * math.pi
reach_sq = 0.75
block_len = 512


def from_behind(x, axis, by):
    devices = lax.axis_size(axis)
    return lax.ppermute(x, axis, [(i, (i + by) % devices) for i in range(devices)])


def shortened(x):
    return jax.tree.map(lambda a: a.astype(jnp.bfloat16) if a.dtype == jnp.float32 else a, x)


def padded(x, sides, width):
    for axis, dim in sides:
        devices, length = (lax.axis_size(axis), x.shape[dim])
        up = [(i, (i + 1) % devices) for i in range(devices)]
        down = [(j, i) for i, j in up]
        last = lax.slice_in_dim(x, length - width, length, axis=dim)
        initial = lax.slice_in_dim(x, 0, width, axis=dim)
        before = lax.ppermute(last, axis, up)
        after = lax.ppermute(initial, axis, down)
        x = jnp.concatenate([before, x, after], axis=dim)
    return x


def by_axis(x, axes):
    return functools.reduce(lax.psum, axes, x)


def phases(local_pos, anchor, reciprocal_points_rescaled):
    absolute = local_pos + anchor[:, None]
    angles = absolute[0][:, None] * reciprocal_points_rescaled[0][None, :]
    angles = angles + absolute[1][:, None] * reciprocal_points_rescaled[1][None, :]
    angles = angles + absolute[2][:, None] * reciprocal_points_rescaled[2][None, :]
    return (jnp.cos(angles).astype(jnp.bfloat16), jnp.sin(angles).astype(jnp.bfloat16))


def structure_terms(cos_part, sin_part, stacked):
    contract = (((0,), (1,)), ((), ()))
    with_cos = lax.dot_general(cos_part, stacked, contract, preferred_element_type=jnp.float32)
    with_sin = lax.dot_general(sin_part, stacked, contract, preferred_element_type=jnp.float32)
    return jnp.concatenate([with_cos, with_sin], axis=1)


def coefficients(totals, filt_rows, norm_atoms, norm_k):
    channels = filt_rows.shape[1]
    cos_struct = totals[:, 0:channels] * norm_atoms
    cos_back = totals[:, channels : 2 * channels] * norm_k
    sin_struct = totals[:, 2 * channels : 3 * channels] * norm_atoms
    sin_back = totals[:, 3 * channels : 4 * channels] * norm_k
    coeffs = jnp.concatenate(
        [
            norm_atoms * filt_rows * cos_back,
            norm_k * filt_rows * cos_struct,
            norm_atoms * filt_rows * sin_back,
            norm_k * filt_rows * sin_struct,
        ],
        axis=1,
    )
    return (coeffs.astype(jnp.bfloat16), cos_struct * cos_back + sin_struct * sin_back)


def ewald_pieces(
    running, piece_rows, start_at, cos_all, sin_all, stacked, reciprocal_points_rescaled
):
    count_rows = piece_rows.shape[0]
    channels = stacked.shape[0] // 2
    cos_part = lax.dynamic_slice_in_dim(cos_all, start_at, count_rows, 1)
    sin_part = lax.dynamic_slice_in_dim(sin_all, start_at, count_rows, 1)
    kv_part = lax.dynamic_slice_in_dim(reciprocal_points_rescaled, start_at, count_rows, 1)
    contract = (((0,), (1,)), ((), ()))
    atom_part = lax.dot_general(
        piece_rows[:, 0:channels], cos_part, contract, preferred_element_type=jnp.float32
    )
    atom_part = atom_part + lax.dot_general(
        piece_rows[:, 2 * channels : 3 * channels],
        sin_part,
        contract,
        preferred_element_type=jnp.float32,
    )
    along_u = lax.dot_general(
        stacked, piece_rows[:, 0 : 2 * channels], contract, preferred_element_type=jnp.float32
    )
    along_v = lax.dot_general(
        stacked,
        piece_rows[:, 2 * channels : 4 * channels],
        contract,
        preferred_element_type=jnp.float32,
    )
    angle_grad = along_v * cos_part.astype(jnp.float32) - along_u * sin_part.astype(jnp.float32)
    pos_part = lax.dot_general(
        kv_part, angle_grad, (((1,), (1,)), ((), ())), precision=lax.Precision.HIGHEST
    )
    return (running[0] + atom_part, running[1] + pos_part)


def species_gains(table, kinds):
    onehot = (kinds[None, :] == jnp.arange(table.shape[0], dtype=jnp.int32)[:, None]).astype(
        jnp.float32
    )
    return lax.dot_general(table, onehot, (((0,), (0,)), ((), ())), precision=lax.Precision.HIGHEST)


def offset_table():
    steps_one = jnp.arange(3, dtype=jnp.float32) - 1.0
    along_x = jnp.broadcast_to(steps_one[:, None, None], (3, 3, 3))
    along_y = jnp.broadcast_to(steps_one[None, :, None], (3, 3, 3))
    along_z = jnp.broadcast_to(steps_one[None, None, :], (3, 3, 3))
    return jnp.stack([along_x, along_y, along_z], axis=-1)


def short_range(ghost_values, ghost_places, neighbour_ids, radial_weights):
    channels = ghost_values.shape[1]
    flat_z = jnp.transpose(ghost_values, (1, 0, 2)).reshape(channels, -1)
    flat_pos = jnp.transpose(ghost_places, (1, 0, 2)).reshape(3, -1)
    near_z = flat_z[:, neighbour_ids]
    near_pos = flat_pos[:, neighbour_ids]
    relative = near_pos - ghost_places[13][:, None, :]
    dist_sq = jnp.sum(relative * relative, axis=0)
    basis_count = radial_weights.shape[0]
    spacing = reach_sq / (basis_count - 1)
    centres = jnp.arange(basis_count, dtype=jnp.float32) * spacing
    radial_basis = jnp.exp(
        -jnp.square((dist_sq[None, :, :] - centres[:, None, None]) / (2.0 * spacing))
    )
    filters = jnp.einsum(
        "bc,bja->cja", radial_weights, radial_basis, precision=lax.Precision.HIGHEST
    )
    agg = jnp.sum(filters * near_z, axis=1) * neighbour_ids.shape[0] ** (-0.5)
    return jax.nn.silu(agg)


def local_backward(ghost_z, ghost_pos, neighbour_ids, distance_kernel, upstream):

    def mapped(ghost_values, ghost_places, radial_weights):
        return short_range(ghost_values, ghost_places, neighbour_ids, radial_weights)

    _, pullback = jax.vjp(mapped, ghost_z.astype(jnp.float32), ghost_pos, distance_kernel)
    return pullback(upstream.astype(jnp.float32))


def fold_gx(grad_z, grad_p, along_axis):
    total_z = lax.index_in_dim(grad_z, 1, along_axis, False)
    total_p = lax.index_in_dim(grad_p, 1, along_axis, False)
    for step_by in (1, -1):
        moved_z, moved_p = (
            from_behind(
                lax.index_in_dim(grad_z, 1 + step_by, along_axis, False).astype(jnp.bfloat16),
                "gx",
                step_by,
            ).astype(jnp.float32),
            from_behind(
                lax.index_in_dim(grad_p, 1 + step_by, along_axis, False).astype(jnp.bfloat16),
                "gx",
                step_by,
            ).astype(jnp.float32),
        )
        total_z = total_z + moved_z
        total_p = total_p + moved_p
    return (total_z, total_p)


def fold_gy(grad_z, grad_p, along_axis):
    total_z = lax.index_in_dim(grad_z, 1, along_axis, False)
    total_p = lax.index_in_dim(grad_p, 1, along_axis, False)
    for step_by in (1, -1):
        moved_z, moved_p = from_behind(
            (
                shortened(lax.index_in_dim(grad_z, 1 + step_by, along_axis, False)),
                shortened(lax.index_in_dim(grad_p, 1 + step_by, along_axis, False)),
            ),
            GY,
            step_by,
        )
        total_z = total_z + moved_z
        total_p = total_p + moved_p
    return (total_z, total_p)


def fold_gz(grad_z, grad_p, along_axis):
    total_z = lax.index_in_dim(grad_z, 1, along_axis, False)
    total_p = lax.index_in_dim(grad_p, 1, along_axis, False)
    for step_by in (1, -1):
        moved_z, moved_p = from_behind(
            (
                lax.index_in_dim(grad_z, 1 + step_by, along_axis, False),
                lax.index_in_dim(grad_p, 1 + step_by, along_axis, False),
            ),
            GZ,
            step_by,
        )
        total_z = total_z + moved_z
        total_p = total_p + moved_p
    return (total_z, total_p)


def shards(
    atom_embedding,
    output_adjoint,
    fractional_coords,
    element_labels,
    adjacent_ghost_entries,
    miller_triples,
    reciprocal_kernel,
    channel_mixing_matrix,
    element_channel_factor,
    distance_kernel,
):
    own_features = atom_embedding[0, 0, 0]
    own_cotangent = output_adjoint[0, 0, 0]
    own_positions = fractional_coords[0, 0, 0]
    channels = own_features.shape[0]
    atom_count = own_features.shape[1]
    reciprocal_total = miller_triples.shape[1]
    device_count = lax.axis_size(GX_GY_GZ)
    norm_atoms = (atom_count * device_count) ** (-0.5)
    norm_k = reciprocal_total ** (-0.5)
    accumulated_entries = jnp.array(
        [lax.axis_size("gx"), lax.axis_size(GY), lax.axis_size(GZ)], jnp.float32
    )
    reciprocal_points_rescaled = (
        miller_triples.astype(jnp.float32) * (circle_angle / accumulated_entries)[:, None]
    )
    anchor = jnp.stack([lax.axis_index("gx"), lax.axis_index(GY), lax.axis_index(GZ)]).astype(
        jnp.float32
    )
    cos_all, sin_all = phases(own_positions, anchor, reciprocal_points_rescaled)
    stacked = jnp.concatenate([own_features, own_cotangent], axis=0)
    share_rows = reciprocal_total // device_count
    share_start = lax.axis_index(GX_GY_GZ) * share_rows
    zeros_pair = (
        jnp.zeros((channels, atom_count), jnp.float32),
        jnp.zeros((3, atom_count), jnp.float32),
    )
    totals = lax.psum(structure_terms(cos_all, sin_all, stacked), GX_GY_GZ)
    coeffs, filter_full = coefficients(totals, reciprocal_kernel, norm_atoms, norm_k)
    filter_share = lax.dynamic_slice_in_dim(filter_full, share_start, share_rows, 0)
    step_rows = min(block_len, reciprocal_total)
    running = zeros_pair
    for offset in range(0, reciprocal_total, step_rows):
        running = ewald_pieces(
            running,
            coeffs[offset : offset + step_rows],
            offset,
            cos_all,
            sin_all,
            stacked,
            reciprocal_points_rescaled,
        )
    ewald_h, ewald_pos = running
    gain_rows = species_gains(element_channel_factor, element_labels[0, 0, 0])
    projected = lax.dot_general(
        channel_mixing_matrix,
        own_features,
        (((0,), (0,)), ((), ())),
        preferred_element_type=jnp.float32,
    )
    z_local = (projected * gain_rows).astype(jnp.bfloat16)
    shifts_all = offset_table().reshape(27, 3)[:, :, None]
    ghost_z = padded(z_local[None, None, None], (("gx", 0), (GY, 1), (GZ, 2)), 1)
    ghost_p = padded(fractional_coords, (("gx", 0), (GY, 1), (GZ, 2)), 1)
    ghost_p = ghost_p.reshape(27, 3, atom_count) + shifts_all
    grad_z, grad_p, grad_radial = local_backward(
        ghost_z.reshape(27, channels, atom_count),
        ghost_p,
        adjacent_ghost_entries[0, 0, 0],
        distance_kernel,
        own_cotangent,
    )
    grad_z = grad_z.reshape(3, 3, 3, channels, atom_count)
    grad_p = grad_p.reshape(3, 3, 3, 3, atom_count)
    grad_z, grad_p = fold_gx(grad_z, grad_p, 0)
    grad_z, grad_p = fold_gy(grad_z, grad_p, 0)
    zgrad, pos_short = fold_gz(grad_z, grad_p, 0)
    zscaled = (zgrad * gain_rows).astype(jnp.bfloat16)
    atom_short = jnp.dot(channel_mixing_matrix, zscaled, preferred_element_type=jnp.float32)
    atom_grad = (own_cotangent.astype(jnp.float32) + ewald_h + atom_short).astype(jnp.bfloat16)
    weight_local = lax.dot_general(
        own_features, zscaled, (((1,), (1,)), ((), ())), preferred_element_type=jnp.float32
    )
    weight_grad, radial_grad = (by_axis(weight_local, GX_GY_GZ), by_axis(grad_radial, GX_GY_GZ))
    position_grad = ewald_pos + pos_short
    return (
        atom_grad[None, None, None],
        position_grad[None, None, None],
        weight_grad,
        radial_grad,
        filter_share,
    )


def solution(mesh):
    finer = Mesh(
        mesh.devices.reshape(mesh.shape["gx"], 4, 4, 2, 2), ("gx", "gy_0", "gy_1", "gz_0", "gz_1")
    )
    in_specs = (
        P("gx", GY, GZ, None, None),
        P("gx", GY, GZ, None, None),
        P("gx", GY, GZ, None, None),
        P("gx", GY, GZ, None),
        P("gx", GY, GZ, None, None),
        P(),
        P(),
        P(),
        P(),
        P(),
    )
    out_specs = (
        P("gx", GY, GZ, None, None),
        P("gx", GY, GZ, None, None),
        P(),
        P(),
        P(GX_GY_GZ, None),
    )
    return jax.shard_map(
        shards, mesh=finer, in_specs=in_specs, out_specs=out_specs, check_vma=False
    )
```

profile of v0, /device:TPU:1, one launch (start us, length us, event | category | flops | bytes accessed | tf_op | source)
XLA Modules:
  0.0 459.9 jit_solution(1965531941578786956)
XLA Ops:
  16.8 15.4 %fusion.113 = f32[2048,128]{0,1:T(8,128)S(1)} fusion(bf16[64,512]{1,0:T(8,128)(2,1)} %bitcast.195, bf16[64,512]{1,0:T(8,128)(2,1)} %bitcast.205, f32[2048]{0:T(1024)S(1)} %bitcast.228, f32[512]{0:T(512)S(1)} %bitcast.237, f32[2048]{0:T(1024)S(1)} %bitcast.231, f32[512]{0:T(512)S(1)} %bitcast.240, f32[2048]{0:T(1024)S(1)} %bitcast.225, f32[512]{0:T(512)S(1)} %bitcast.234), kind=kOutput, calls=%fused_computation.203 | convolution fusion | flops 274989056 | bytes 1210368 | tf_op jit(solution)/shard_map/dot_general | solution.py:56
  32.2 14.5 %fusion.114 = f32[2048,128]{0,1:T(8,128)S(1)} fusion(bf16[64,512]{1,0:T(8,128)(2,1)S(1)} %bitcast.196, bf16[64,512]{1,0:T(8,128)(2,1)S(1)} %bitcast.206, f32[2048]{0:T(1024)S(1)} %bitcast.229, f32[512]{0:T(512)S(1)} %bitcast.238, f32[2048]{0:T(1024)S(1)} %bitcast.232, f32[512]{0:T(512)S(1)} %bitcast.241, f32[2048]{0:T(1024)S(1)} %bitcast.226, ...), kind=kOutput, calls=%fused_computation.204 | convolution fusion | flops 274989056 | bytes 1210368 | tf_op jit(solution)/shard_map/dot_general | solution.py:57
  48.3 17.0 %sine_convert_fusion = (bf16[512,2048]{1,0:T(8,128)(2,1)}, bf16[512,2048]{1,0:T(8,128)(2,1)}) fusion(f32[2048]{0:T(1024)S(1)} %bitcast.230, f32[512]{0:T(512)S(1)} %bitcast.239, f32[2048]{0:T(1024)S(1)} %bitcast.233, f32[512]{0:T(512)S(1)} %bitcast.242, f32[2048]{0:T(1024)S(1)} %bitcast.227, f32[512]{0:T(512)S(1)} %bitcast.236), kind=kLoop, calls=%fused_computation.7 | loop fusion | flops 7340032 | bytes 4225024 | tf_op jit(solution)/shard_map/convert_element_type | solution.py:51
  65.4 7.0 %collective-permute-start.3 = (f32[3,1,1,3,512]{4,2,3,1,0:T(1,128)S(1)}, f32[3,1,1,3,512]{4,2,3,1,0:T(1,128)S(1)}, u32[]{:S(2)}, u32[]{:S(2)}) collective-permute-start(f32[3,1,1,3,512]{4,2,3,1,0:T(1,128)S(1)} %constant_dynamic-update-slice_fusion), channel_id=1, source_target_pairs={{4,0},{8,4},{12,8},{16,12},{20,16},{24,20},{28,24},{32,28},{36,32}... | collective-permute-start | bytes 55304 | tf_op jit(solution)/shard_map/ppermute | solution.py:37
  73.3 5.7 %collective-permute-done.2 = f32[3,1,1,3,512]{4,2,3,1,0:T(1,128)S(1)} collective-permute-done((f32[3,1,1,3,512]{4,2,3,1,0:T(1,128)S(1)}, f32[3,1,1,3,512]{4,2,3,1,0:T(1,128)S(1)}, u32[]{:S(2)}, u32[]{:S(2)}) %collective-permute-start.2) | collective-permute-done | bytes 18464 | tf_op jit(solution)/shard_map/ppermute | solution.py:36
  79.0 3.3 collective-permute-start.5
  82.3 4.2 collective-permute-start.4
  91.7 4.5 collective-permute-done.8
  96.4 5.6 %collective-permute-start.10 = (bf16[3,3,1,64,512]{4,3,2,1,0:T(8,128)(2,1)S(1)}, bf16[3,3,1,64,512]{4,3,2,1,0:T(8,128)(2,1)S(1)}, u32[]{:S(2)}, u32[]{:S(2)}) collective-permute-start(bf16[3,3,1,64,512]{4,3,2,1,0:T(8,128)(2,1)S(1)} %pad_maximum_fusion.2), channel_id=1, source_target_pairs={{0,1},{1,2},{2,3},{3,0},{4,5},{5,6},{6,7},{7,4},{8,9},{9,10},{10,1... | collective-permute-start | bytes 1769480 | tf_op jit(solution)/shard_map/ppermute | solution.py:36
  102.3 4.1 copy.37
  106.5 30.7 %gather_fusion = f32[8192,3]{1,0:T(8,128)} fusion(f32[3,13824]{0,1:T(8,128)} %bitcast.194, s32[8192]{0:T(1024)S(1)} %broadcast_clamp_fusion), kind=kCustom, calls=%fused_computation | custom fusion | bytes 229376 | tf_op jit(solution)/shard_map/jvp()/gather | solution.py:133
  137.2 3.9 multiply_reduce_fusion
  142.0 4.4 copy.39
  146.5 33.4 %gather_fusion.1 = f32[8192,64]{1,0:T(8,128)} fusion(f32[64,13824]{0,1:T(8,128)} %bitcast.187, s32[8192]{0:T(1024)} %copy-done.16), kind=kCustom, calls=%fused_computation.1 | custom fusion | bytes 4227072 | tf_op jit(solution)/shard_map/jvp()/gather | solution.py:132
  179.9 2.9 copy.41
  187.2 3.1 add_multiply_fusion
  196.3 47.7 %scatter_custom_fusion = f32[64,13824]{0,1:T(8,128)} fusion(s32[8192]{0:T(1024)} %bitcast.221, f32[8192,64]{1,0:T(8,128)} %bitcast.216, f32[]{:T(128)} %constant.22.clone.1), kind=kCustom, calls=%fused_computation.13 | custom fusion | flops 524288 | bytes 3539456 | tf_op jit(solution)/shard_map/transpose(jvp())/scatter-add | solution.py:132
  244.0 4.7 %copy.44 = f32[64,27,512]{2,0,1:T(8,128)S(1)} copy(f32[64,27,512]{0,2,1:T(8,128)} %bitcast.189) | data formatting | bytes 7077888 | tf_op jit(solution)/shard_map/transpose(jvp())/reshape | solution.py:130
  250.2 47.6 %scatter_custom_fusion.1 = f32[3,13824]{0,1:T(8,128)} fusion(s32[8192]{0:T(1024)} %bitcast.222, f32[8192,3]{1,0:T(8,128)} %bitcast.192, f32[]{:T(128)} %constant.22.clone.1), kind=kCustom, calls=%fused_computation.11 | custom fusion | flops 24576 | bytes 166400 | tf_op jit(solution)/shard_map/transpose(jvp())/scatter-add | solution.py:133
  297.8 7.2 %fusion.116 = (bf16[27,3,512]{1,2,0:T(8,128)(2,1)S(1)}, f32[27,3,512]{1,2,0:T(8,128)}) fusion(f32[27,3,512]{1,2,0:T(8,128)} %bitcast.188, f32[1,3,512]{1,2,0:T(8,128)} %negate_bitcast_fusion), kind=kLoop, calls=%fused_computation.206 | loop fusion | flops 82944 | bytes 420864 | tf_op jit(solution)/shard_map/convert.6
  315.9 3.3 slice.274
  319.2 3.0 copy.45
  323.2 5.4 %collective-permute-start.21 = (bf16[3,3,512]{2,1,0:T(4,128)(2,1)S(1)}, bf16[3,3,512]{2,1,0:T(4,128)(2,1)S(1)}, u32[]{:S(2)}, u32[]{:S(2)}) collective-permute-start(bf16[3,3,512]{2,1,0:T(4,128)(2,1)S(1)} %get-tuple-element.53), channel_id=1, source_target_pairs={{0,60},{4,0},{8,4},{12,8},{16,12},{20,16},{24,20},{28,24},{32,28},... | collective-permute-start | bytes 27656 | tf_op jit(solution)/shard_map/ppermute | solution.py:22
  328.6 4.0 fusion.27
  355.5 5.4 %collective-permute-start.15 = (bf16[3,64,512]{2,1,0:T(8,128)(2,1)S(1)}, bf16[3,64,512]{2,1,0:T(8,128)(2,1)S(1)}, u32[]{:S(2)}, u32[]{:S(2)}) collective-permute-start(bf16[3,64,512]{2,1,0:T(8,128)(2,1)S(1)} %get-tuple-element.49), channel_id=1, source_target_pairs={{0,60},{4,0},{8,4},{12,8},{16,12},{20,16},{24,20},{28,24},{32,28},... | collective-permute-start | bytes 589832 | tf_op jit(solution)/shard_map/ppermute | solution.py:22
  364.0 7.8 %collective-permute-start.16 = (f32[64,512]{1,0:T(8,128)S(1)}, f32[64,512]{1,0:T(8,128)S(1)}, u32[]{:S(2)}, u32[]{:S(2)}) collective-permute-start(f32[64,512]{1,0:T(8,128)S(1)} %get-tuple-element.50), channel_id=1, source_target_pairs={{0,1},{1,2},{2,3},{3,0},{4,5},{5,6},{6,7},{7,4},{8,9},{9,10},{10,1... | collective-permute-start | bytes 393224 | tf_op jit(solution)/shard_map/ppermute | solution.py:22
  373.8 6.4 %collective-permute-done.17 = f32[64,512]{1,0:T(8,128)S(1)} collective-permute-done((f32[64,512]{1,0:T(8,128)S(1)}, f32[64,512]{1,0:T(8,128)S(1)}, u32[]{:S(2)}, u32[]{:S(2)}) %collective-permute-start.17) | collective-permute-done | bytes 131104 | tf_op jit(solution)/shard_map/ppermute | solution.py:22
  381.1 14.1 %all-reduce.3 = (f32[64,64]{0,1:T(8,128)S(1)}, f32[16,64]{1,0:T(8,128)S(1)}) all-reduce(f32[64,64]{0,1:T(8,128)S(1)} %convolution_bitcast_fusion.2, f32[16,64]{1,0:T(8,128)S(1)} %copy-done.20), channel_id=1, replica_groups=mesh['gx'=4,'gy_0'=4,'gy_1'=4,'gz_0'=2,'gz_1'=2] {'gx'}, use_global_device_ids=true, to_apply=%region_7.8 | all-reduce | flops 5120 | bytes 40960 | tf_op jit(solution)/shard_map/psum | solution.py:43
  395.2 12.7 %all-reduce.2 = (f32[64,64]{0,1:T(8,128)S(1)}, f32[16,64]{1,0:T(8,128)S(1)}) all-reduce(f32[64,64]{0,1:T(8,128)S(1)} %get-tuple-element.24, f32[16,64]{1,0:T(8,128)S(1)} %get-tuple-element.25), channel_id=1, replica_groups=mesh['gx'=4,'gy_0'=4,'gy_1'=4,'gz_0'=2,'gz_1'=2] {'gy_0'}, use_global_device_ids=true, to_apply=%region_8.9 | all-reduce | flops 5120 | bytes 40960 | tf_op jit(solution)/shard_map/psum | solution.py:43
  407.9 17.5 %all-reduce.1 = (f32[64,64]{0,1:T(8,128)S(1)}, f32[16,64]{1,0:T(8,128)S(1)}) all-reduce(f32[64,64]{0,1:T(8,128)S(1)} %get-tuple-element.22, f32[16,64]{1,0:T(8,128)S(1)} %get-tuple-element.23), channel_id=1, replica_groups=mesh['gx'=4,'gy_0'=4,'gy_1'=4,'gz_0'=2,'gz_1'=2] {'gy_1'}, use_global_device_ids=true, to_apply=%region_9.10 | all-reduce | flops 5120 | bytes 40960 | tf_op jit(solution)/shard_map/psum | solution.py:43
  425.4 14.1 %all-reduce.5 = (f32[64,64]{0,1:T(8,128)S(1)}, f32[16,64]{1,0:T(8,128)S(1)}) all-reduce(f32[64,64]{0,1:T(8,128)S(1)} %get-tuple-element.20, f32[16,64]{1,0:T(8,128)S(1)} %get-tuple-element.21), channel_id=1, replica_groups=mesh['gx'=4,'gy_0'=4,'gy_1'=4,'gz_0'=2,'gz_1'=2] {'gz_0'}, use_global_device_ids=true, to_apply=%region_10.11 | all-reduce | flops 5120 | bytes 40960 | tf_op jit(solution)/shard_map/psum | solution.py:43
  439.6 12.6 %all-reduce.4 = (f32[64,64]{0,1:T(8,128)S(1)}, f32[16,64]{1,0:T(8,128)}) all-reduce(f32[64,64]{0,1:T(8,128)S(1)} %get-tuple-element.28, f32[16,64]{1,0:T(8,128)S(1)} %get-tuple-element.29), channel_id=1, replica_groups=mesh['gx'=4,'gy_0'=4,'gy_1'=4,'gz_0'=2,'gz_1'=2] {'gz_1'}, use_global_device_ids=true, to_apply=%region_11.12 | all-reduce | flops 5120 | bytes 40960 | tf_op jit(solution)/shard_map/psum | solution.py:43
  (174 shorter events, 71.7 us)
Async XLA Ops:
  7.2 331.0 %all-reduce.8.cloned.1.call-start = ((), (), s32[]{:S(2)}) async-start(), calls=%async_computation | async-start | bytes 4194304 | tf_op jit(solution)/shard_map/psum | solution.py:251
  7.2 58.2 %collective-permute-start = (f32[1,1,1,3,512]{4,2,3,1,0:T(1,128)}, f32[1,1,1,3,512]{4,2,3,1,0:T(1,128)S(1)}, u32[]{:S(2)}, u32[]{:S(2)}) collective-permute-start(f32[1,1,1,3,512]{4,2,3,1,0:T(1,128)} %param.13), channel_id=1, source_target_pairs={{0,64},{64,128},{128,192},{192,0},{1,65},{65,129},{129,193},{193,1... | collective-permute-start | bytes 18440 | tf_op jit(solution)/shard_map/ppermute | solution.py:36
  9.3 56.1 %collective-permute-start.1 = (f32[1,1,1,3,512]{4,2,3,1,0:T(1,128)}, f32[1,1,1,3,512]{4,2,3,1,0:T(1,128)S(1)}, u32[]{:S(2)}, u32[]{:S(2)}) collective-permute-start(f32[1,1,1,3,512]{4,2,3,1,0:T(1,128)} %param.13), channel_id=1, source_target_pairs={{64,0},{128,64},{192,128},{0,192},{65,1},{129,65},{193,129},{1,193... | collective-permute-start | bytes 18440 | tf_op jit(solution)/shard_map/ppermute | solution.py:37
  13.3 73.2 %collective-permute-start.7 = (bf16[1,1,1,64,512]{4,3,2,1,0:T(8,128)(2,1)S(1)}, bf16[1,1,1,64,512]{4,3,2,1,0:T(8,128)(2,1)S(1)}, u32[]{:S(2)}, u32[]{:S(2)}) collective-permute-start(bf16[1,1,1,64,512]{4,3,2,1,0:T(8,128)(2,1)S(1)} %fusion.26), channel_id=1, source_target_pairs={{64,0},{128,64},{192,128},{0,192},{65,1},{129,65},{193,129},{1,193... | collective-permute-start | bytes 196616 | tf_op jit(solution)/shard_map/ppermute | solution.py:37
  14.8 71.7 %collective-permute-start.6 = (bf16[1,1,1,64,512]{4,3,2,1,0:T(8,128)(2,1)S(1)}, bf16[1,1,1,64,512]{4,3,2,1,0:T(8,128)(2,1)S(1)}, u32[]{:S(2)}, u32[]{:S(2)}) collective-permute-start(bf16[1,1,1,64,512]{4,3,2,1,0:T(8,128)(2,1)S(1)} %fusion.26), channel_id=1, source_target_pairs={{0,64},{64,128},{128,192},{192,0},{1,65},{65,129},{129,193},{193,1... | collective-permute-start | bytes 196616 | tf_op jit(solution)/shard_map/ppermute | solution.py:36
  16.8 29.9 %copy-start.17 = (f32[3,2048]{1,0:T(4,128)}, f32[3,2048]{1,0:T(4,128)S(1)}, u32[]{:S(2)}) copy-start(f32[3,2048]{1,0:T(4,128)S(1)} %convert_multiply_fusion.2) | copy-start | bytes 73732
  48.2 17.2 %copy-start.22 = (f32[1,1,1,3,512]{4,2,3,1,0:T(1,128)S(1)}, f32[1,1,1,3,512]{4,2,3,1,0:T(1,128)}, u32[]{:S(2)}) copy-start(f32[1,1,1,3,512]{4,2,3,1,0:T(1,128)} %param.13) | copy-start | bytes 18436
  65.3 21.2 %copy-start.19 = (s32[2,4,8,128]{3,1,2,0:T(4,128)}, s32[2,4,8,128]{3,1,2,0:T(4,128)S(1)}, u32[]{:S(2)}) copy-start(s32[2,4,8,128]{3,1,2,0:T(4,128)S(1)} %copy.57) | copy-start | bytes 98308
  65.4 41.1 %copy-start.16 = (s32[8192]{0:T(1024)}, s32[8192]{0:T(1024)S(1)}, u32[]{:S(2)}) copy-start(s32[8192]{0:T(1024)S(1)} %broadcast_clamp_fusion) | copy-start | bytes 98308
  65.4 7.9 %collective-permute-start.3 = (f32[3,1,1,3,512]{4,2,3,1,0:T(1,128)S(1)}, f32[3,1,1,3,512]{4,2,3,1,0:T(1,128)S(1)}, u32[]{:S(2)}, u32[]{:S(2)}) collective-permute-start(f32[3,1,1,3,512]{4,2,3,1,0:T(1,128)S(1)} %constant_dynamic-update-slice_fusion), channel_id=1, source_target_pairs={{4,0},{8,4},{12,8},{16,12},{20,16},{24,20},{28,24},{32,28},{36,32}... | collective-permute-start | bytes 55304 | tf_op jit(solution)/shard_map/ppermute | solution.py:37
  72.4 6.5 %collective-permute-start.2 = (f32[3,1,1,3,512]{4,2,3,1,0:T(1,128)S(1)}, f32[3,1,1,3,512]{4,2,3,1,0:T(1,128)S(1)}, u32[]{:S(2)}, u32[]{:S(2)}) collective-permute-start(f32[3,1,1,3,512]{4,2,3,1,0:T(1,128)S(1)} %constant_dynamic-update-slice_fusion), channel_id=1, source_target_pairs={{0,4},{4,8},{8,12},{12,16},{16,20},{20,24},{24,28},{28,32},{32,36}... | collective-permute-start | bytes 55304 | tf_op jit(solution)/shard_map/ppermute | solution.py:36
  79.0 10.1 %collective-permute-start.5 = (f32[3,3,1,3,512]{4,2,3,1,0:T(1,128)S(1)}, f32[3,3,1,3,512]{4,2,3,1,0:T(1,128)S(1)}, u32[]{:S(2)}, u32[]{:S(2)}) collective-permute-start(f32[3,3,1,3,512]{4,2,3,1,0:T(1,128)S(1)} %pad_maximum_fusion.10), channel_id=1, source_target_pairs={{1,0},{2,1},{3,2},{0,3},{5,4},{6,5},{7,6},{4,7},{9,8},{10,9},{11,1... | collective-permute-start | bytes 165896 | tf_op jit(solution)/shard_map/ppermute | solution.py:37
  82.3 6.8 %collective-permute-start.4 = (f32[3,3,1,3,512]{4,2,3,1,0:T(1,128)S(1)}, f32[3,3,1,3,512]{4,2,3,1,0:T(1,128)S(1)}, u32[]{:S(2)}, u32[]{:S(2)}) collective-permute-start(f32[3,3,1,3,512]{4,2,3,1,0:T(1,128)S(1)} %pad_maximum_fusion.10), channel_id=1, source_target_pairs={{0,1},{1,2},{2,3},{3,0},{4,5},{5,6},{6,7},{7,4},{8,9},{9,10},{10,1... | collective-permute-start | bytes 165896 | tf_op jit(solution)/shard_map/ppermute | solution.py:36
  86.5 5.2 %collective-permute-start.9 = (bf16[3,1,1,64,512]{4,3,2,1,0:T(8,128)(2,1)S(1)}, bf16[3,1,1,64,512]{4,3,2,1,0:T(8,128)(2,1)S(1)}, u32[]{:S(2)}, u32[]{:S(2)}) collective-permute-start(bf16[3,1,1,64,512]{4,3,2,1,0:T(8,128)(2,1)S(1)} %pad_maximum_fusion.4), channel_id=1, source_target_pairs={{4,0},{8,4},{12,8},{16,12},{20,16},{24,20},{28,24},{32,28},{36,32}... | collective-permute-start | bytes 589832 | tf_op jit(solution)/shard_map/ppermute | solution.py:37
  86.6 9.6 %collective-permute-start.8 = (bf16[3,1,1,64,512]{4,3,2,1,0:T(8,128)(2,1)S(1)}, bf16[3,1,1,64,512]{4,3,2,1,0:T(8,128)(2,1)S(1)}, u32[]{:S(2)}, u32[]{:S(2)}) collective-permute-start(bf16[3,1,1,64,512]{4,3,2,1,0:T(8,128)(2,1)S(1)} %pad_maximum_fusion.4), channel_id=1, source_target_pairs={{0,4},{4,8},{8,12},{12,16},{16,20},{20,24},{24,28},{28,32},{32,36}... | collective-permute-start | bytes 589832 | tf_op jit(solution)/shard_map/ppermute | solution.py:36
  96.3 44.9 %collective-permute-start.11 = (bf16[3,3,1,64,512]{4,3,2,1,0:T(8,128)(2,1)S(1)}, bf16[3,3,1,64,512]{4,3,2,1,0:T(8,128)(2,1)S(1)}, u32[]{:S(2)}, u32[]{:S(2)}) collective-permute-start(bf16[3,3,1,64,512]{4,3,2,1,0:T(8,128)(2,1)S(1)} %pad_maximum_fusion.2), channel_id=1, source_target_pairs={{1,0},{2,1},{3,2},{0,3},{5,4},{6,5},{7,6},{4,7},{9,8},{10,9},{11,1... | collective-permute-start | bytes 1769480 | tf_op jit(solution)/shard_map/ppermute | solution.py:37
  96.4 44.8 %collective-permute-start.10 = (bf16[3,3,1,64,512]{4,3,2,1,0:T(8,128)(2,1)S(1)}, bf16[3,3,1,64,512]{4,3,2,1,0:T(8,128)(2,1)S(1)}, u32[]{:S(2)}, u32[]{:S(2)}) collective-permute-start(bf16[3,3,1,64,512]{4,3,2,1,0:T(8,128)(2,1)S(1)} %pad_maximum_fusion.2), channel_id=1, source_target_pairs={{0,1},{1,2},{2,3},{3,0},{4,5},{5,6},{6,7},{7,4},{8,9},{9,10},{10,1... | collective-permute-start | bytes 1769480 | tf_op jit(solution)/shard_map/ppermute | solution.py:36
  102.2 35.0 %copy-start.10 = (f32[1,3,512]{1,2,0:T(8,128)}, f32[1,3,512]{1,2,0:T(8,128)S(1)}, u32[]{:S(2)}) copy-start(f32[1,3,512]{1,2,0:T(8,128)S(1)} %copy.51) | copy-start | bytes 18436
  311.3 10.9 %collective-permute-start.19 = (bf16[3,3,3,512]{3,2,1,0:T(4,128)(2,1)}, bf16[3,3,3,512]{3,2,1,0:T(4,128)(2,1)}, u32[]{:S(2)}, u32[]{:S(2)}) collective-permute-start(bf16[3,3,3,512]{3,2,1,0:T(4,128)(2,1)} %bitcast.224), channel_id=1, source_target_pairs={{0,192},{64,0},{128,64},{192,128},{1,193},{65,1},{129,65},{193,129... | collective-permute-start | bytes 82952 | tf_op jit(solution)/shard_map/ppermute | solution.py:22
  313.6 8.6 %collective-permute-start.18 = (bf16[3,3,3,512]{3,2,1,0:T(4,128)(2,1)}, bf16[3,3,3,512]{3,2,1,0:T(4,128)(2,1)}, u32[]{:S(2)}, u32[]{:S(2)}) collective-permute-start(bf16[3,3,3,512]{3,2,1,0:T(4,128)(2,1)} %bitcast.223), channel_id=1, source_target_pairs={{0,64},{64,128},{128,192},{192,0},{1,65},{65,129},{129,193},{193,1... | collective-permute-start | bytes 82952 | tf_op jit(solution)/shard_map/ppermute | solution.py:22
  323.1 13.3 %collective-permute-start.20 = (bf16[3,3,512]{2,1,0:T(4,128)(2,1)S(1)}, bf16[3,3,512]{2,1,0:T(4,128)(2,1)S(1)}, u32[]{:S(2)}, u32[]{:S(2)}) collective-permute-start(bf16[3,3,512]{2,1,0:T(4,128)(2,1)S(1)} %get-tuple-element.52), channel_id=1, source_target_pairs={{0,4},{4,8},{8,12},{12,16},{16,20},{20,24},{24,28},{28,32},{32,36}... | collective-permute-start | bytes 27656 | tf_op jit(solution)/shard_map/ppermute | solution.py:22
  323.2 13.2 %collective-permute-start.21 = (bf16[3,3,512]{2,1,0:T(4,128)(2,1)S(1)}, bf16[3,3,512]{2,1,0:T(4,128)(2,1)S(1)}, u32[]{:S(2)}, u32[]{:S(2)}) collective-permute-start(bf16[3,3,512]{2,1,0:T(4,128)(2,1)S(1)} %get-tuple-element.53), channel_id=1, source_target_pairs={{0,60},{4,0},{8,4},{12,8},{16,12},{20,16},{24,20},{28,24},{32,28},... | collective-permute-start | bytes 27656 | tf_op jit(solution)/shard_map/ppermute | solution.py:22
  333.8 19.8 %collective-permute-start.13 = (bf16[3,3,64,512]{3,2,1,0:T(8,128)(2,1)}, bf16[3,3,64,512]{3,2,1,0:T(8,128)(2,1)S(1)}, u32[]{:S(2)}, u32[]{:S(2)}) collective-permute-start(bf16[3,3,64,512]{3,2,1,0:T(8,128)(2,1)} %bitcast.33), channel_id=1, source_target_pairs={{0,192},{64,0},{128,64},{192,128},{1,193},{65,1},{129,65},{193,129... | collective-permute-start | bytes 1769480 | tf_op jit(solution)/shard_map/ppermute | solution.py:22
  336.4 17.2 %collective-permute-start.12 = (bf16[3,3,64,512]{3,2,1,0:T(8,128)(2,1)}, bf16[3,3,64,512]{3,2,1,0:T(8,128)(2,1)}, u32[]{:S(2)}, u32[]{:S(2)}) collective-permute-start(bf16[3,3,64,512]{3,2,1,0:T(8,128)(2,1)} %bitcast.32), channel_id=1, source_target_pairs={{0,64},{64,128},{128,192},{192,0},{1,65},{65,129},{129,193},{193,1... | collective-permute-start | bytes 1769480 | tf_op jit(solution)/shard_map/ppermute | solution.py:22
  336.5 13.0 %collective-permute-start.22 = (f32[3,512]{1,0:T(4,128)S(1)}, f32[3,512]{1,0:T(4,128)S(1)}, u32[]{:S(2)}, u32[]{:S(2)}) collective-permute-start(f32[3,512]{1,0:T(4,128)S(1)} %get-tuple-element.59), channel_id=1, source_target_pairs={{0,1},{1,2},{2,3},{3,0},{4,5},{5,6},{6,7},{7,4},{8,9},{9,10},{10,1... | collective-permute-start | bytes 18440 | tf_op jit(solution)/shard_map/ppermute | solution.py:22
  338.2 11.3 %collective-permute-start.23 = (f32[3,512]{1,0:T(4,128)S(1)}, f32[3,512]{1,0:T(4,128)S(1)}, u32[]{:S(2)}, u32[]{:S(2)}) collective-permute-start(f32[3,512]{1,0:T(4,128)S(1)} %get-tuple-element.60), channel_id=1, source_target_pairs={{0,3},{1,0},{2,1},{3,2},{4,7},{5,4},{6,5},{7,6},{8,11},{9,8},{10,9... | collective-permute-start | bytes 18440 | tf_op jit(solution)/shard_map/ppermute | solution.py:22
  353.6 26.5 %copy-start.14 = (f32[64,512]{1,0:T(8,128)S(1)}, f32[64,512]{1,0:T(8,128)}, u32[]{:S(2)}) copy-start(f32[64,512]{1,0:T(8,128)} %copy-done.13) | copy-start | bytes 393220
  355.4 25.7 %copy-start.20 = (f32[16,64]{1,0:T(8,128)S(1)}, f32[16,64]{1,0:T(8,128)}, u32[]{:S(2)}) copy-start(f32[16,64]{1,0:T(8,128)} %fusion.27) | copy-start | bytes 12292
  355.4 8.5 %collective-permute-start.14 = (bf16[3,64,512]{2,1,0:T(8,128)(2,1)S(1)}, bf16[3,64,512]{2,1,0:T(8,128)(2,1)S(1)}, u32[]{:S(2)}, u32[]{:S(2)}) collective-permute-start(bf16[3,64,512]{2,1,0:T(8,128)(2,1)S(1)} %get-tuple-element.48), channel_id=1, source_target_pairs={{0,4},{4,8},{8,12},{12,16},{16,20},{20,24},{24,28},{28,32},{32,36}... | collective-permute-start | bytes 589832 | tf_op jit(solution)/shard_map/ppermute | solution.py:22
  355.5 8.4 %collective-permute-start.15 = (bf16[3,64,512]{2,1,0:T(8,128)(2,1)S(1)}, bf16[3,64,512]{2,1,0:T(8,128)(2,1)S(1)}, u32[]{:S(2)}, u32[]{:S(2)}) collective-permute-start(bf16[3,64,512]{2,1,0:T(8,128)(2,1)S(1)} %get-tuple-element.49), channel_id=1, source_target_pairs={{0,60},{4,0},{8,4},{12,8},{16,12},{20,16},{24,20},{28,24},{32,28},... | collective-permute-start | bytes 589832 | tf_op jit(solution)/shard_map/ppermute | solution.py:22
  364.0 9.7 %collective-permute-start.16 = (f32[64,512]{1,0:T(8,128)S(1)}, f32[64,512]{1,0:T(8,128)S(1)}, u32[]{:S(2)}, u32[]{:S(2)}) collective-permute-start(f32[64,512]{1,0:T(8,128)S(1)} %get-tuple-element.50), channel_id=1, source_target_pairs={{0,1},{1,2},{2,3},{3,0},{4,5},{5,6},{6,7},{7,4},{8,9},{9,10},{10,1... | collective-permute-start | bytes 393224 | tf_op jit(solution)/shard_map/ppermute | solution.py:22
  371.8 8.3 %collective-permute-start.17 = (f32[64,512]{1,0:T(8,128)S(1)}, f32[64,512]{1,0:T(8,128)S(1)}, u32[]{:S(2)}, u32[]{:S(2)}) collective-permute-start(f32[64,512]{1,0:T(8,128)S(1)} %get-tuple-element.51), channel_id=1, source_target_pairs={{0,3},{1,0},{2,1},{3,2},{4,7},{5,4},{6,5},{7,6},{8,11},{9,8},{10,9... | collective-permute-start | bytes 393224 | tf_op jit(solution)/shard_map/ppermute | solution.py:22
  (18 other events, 91.4 us)
Sparse Core Ops, SparseCore 0:
  48.4 283.5 all-reduce.7
where the time goes:
time: 464 us; the launch traced here: 460 us
  other arithmetic  142 us (31%)
  local copies, waits for them, and re-layouts  103 us (22%)
  blocking collectives  71 us (15%)
  matrix products  53.5 us (12%)
  starting transfers between devices  52.6 us (11%)
  waiting for transfers between devices  23 us (5%)
  between operations  15 us (3%)
    psum x5, blocking collectives, by_axis(): return functools.reduce(lax.psum, axes, x)  71 us
    scatter-add x1, other arithmetic, short_range(): near_z = flat_z[:, neighbour_ids]  47.7 us
    scatter-add x1, other arithmetic, short_range(): near_pos = flat_pos[:, neighbour_ids]  47.6 us
    gather x2, local copies, waits for them, and re-layouts, short_range(): near_z = flat_z[:, neighbour_ids]  36.3 us
    gather x1, local copies, waits for them, and re-layouts, short_range(): near_pos = flat_pos[:, neighbour_ids]  30.7 us
    ppermute x12, starting transfers between devices, from_behind(): lax.ppermute(x, axis, [(i, (i + by) % devices) for i in range(devices)])  25.3 us
    convert_element_type x1, other arithmetic, phases(): jnp.sin(angles).astype(jnp.bfloat16)  17 us
    dot_general x1, matrix products, structure_terms(): lax.dot_general(cos_part, stacked, contract, preferred_element_type=jnp.f...  15.4 us
  transfers between devices with their start and end apart: 25, of which 7 were waited for; matrix products, arithmetic and copies ran while one was open for 64% of the time, Pallas kernels for 0%

commit v1 on v0

v1 whole, which is shorter than its diff:
```python
import functools
import math

import jax
import jax.numpy as jnp
from jax import lax
from jax.experimental import pallas as pl
from jax.experimental.pallas import tpu as pltpu
from jax.sharding import Mesh
from jax.sharding import PartitionSpec as P

AXES = ("gx", "gy_0", "gy_1", "gz_0", "gz_1")
GY = ("gy_0", "gy_1")
GZ = ("gz_0", "gz_1")
MESH = pl.DeviceIdType.MESH
f32, bf16, i32 = jnp.float32, jnp.bfloat16, jnp.int32

CH = 64
ATOMS = 512
NBR = 16
NB = 16
ROWS = 8
SEG = 768
FEAT = 80
reach_sq = 0.75

COS = (
    0.9999999890590228,
    -19.739204499454026,
    64.93911745990036,
    -85.45013953095037,
    60.16763095136588,
    -25.96759924965491,
    6.528658162567069,
)
SIN = (
    6.283185302511503,
    -41.34170040531769,
    81.60513138580204,
    -76.7030153539128,
    42.02592698618416,
    -14.899846668691637,
    3.238137510515757,
)

SLOTS = [(ox, oy, oz) for ox in (-1, 0, 1) for oy in (-1, 0, 1) for oz in (-1, 0, 1)]
FACES = [o for o in SLOTS if sum(map(abs, o)) == 1]
EDGES = [o for o in SLOTS if sum(map(abs, o)) == 2]
CORNERS = [o for o in SLOTS if sum(map(abs, o)) == 3]
GHOSTS = FACES + EDGES + CORNERS


def base_block(o):
    if o in FACES:
        return 32 + 9 * FACES.index(o)
    if o in EDGES:
        return 32 + 54 + 3 * EDGES.index(o)
    if o in CORNERS:
        return 32 + 54 + 36 + CORNERS.index(o)
    return 0


def poly(coef, x):
    acc = jnp.full_like(x, coef[-1])
    for c in coef[-2::-1]:
        acc = acc * x + c
    return acc


def split2(x):
    hi = x.astype(bf16)
    return hi, (x - hi.astype(f32)).astype(bf16)


def dot_nn(a, b):
    return jnp.dot(a, b, preferred_element_type=f32)


def dot_nt(a, b):
    return lax.dot_general(a, b, (((1,), (1,)), ((), ())), preferred_element_type=f32)


def pick(ref, o):
    return ref.at[tuple(slice(None) if c == 0 else 1 - c for c in o)]


def region(o, faces, edges, corners):
    if o in FACES:
        return faces.at[FACES.index(o)]
    if o in EDGES:
        return edges.at[EDGES.index(o)]
    return corners.at[CORNERS.index(o)]


def kernel(
    sizes,
    h_ref, dy_ref, pos_ref, lab_ref, idx_ref, mil_ref, kf_ref, mix_ref, gain_ref, rad_ref,
    atom_out, pos_out, weight_out, radial_out, filter_out,
    cs, tot, arr,
    feat, feat5, gf, ge, gc,
    meta, onehot, near, filt, basis_s, rel_s, dgs, agg_s, grad_s, own_s, ownpos_s, u_s, drad_s,
    sf, se, sc, rf, re, rc,
    rec_a, a_bf, rec_b, sum_b, rec_c, g1,
    m9_s, p9_s, st_s, stt_s, gains_s, ew_s, ep_s, kf_s, mi_s, tab_s,
    ar_l, ar_r, ar_x, ar_z, ar_o,
    kf_sem, gs, gr, bs, br, cs_s, cs_r, xs, xr, zs, zr, azs, azr, axs, axr, acs, acr,
    rcs, rcr, rxs, rxr, rzs, rzr, ros, ror,
):
    nx, nl, ny, nh, nc = sizes
    x, zl, y, zh, co = (lax.axis_index(a) for a in AXES)
    devices = nx * nl * ny * nh * nc
    gy, gz = zl * ny + y, zh * nc + co
    n_gy, n_gz = nl * ny, nh * nc
    owner = ((x * nl + zl) * ny + y) * nh * nc + zh * nc + co
    norm_atoms = (ATOMS * devices) ** (-0.5)
    norm_k = (ROWS * devices) ** (-0.5)

    def brick(ox, oy, oz):
        bx = lax.rem(x + (ox + nx), nx)
        by = lax.rem(gy + (oy + n_gy), n_gy)
        bz = lax.rem(gz + (oz + n_gz), n_gz)
        return (bx, by // ny, lax.rem(by, ny), bz // nc, lax.rem(bz, nc))

    xy_steps = [(i, j) for i in range(nx) for j in range(ny) if (i, j) != (0, 0)]
    z_steps = [(i, j) for i in range(nh) for j in range(nl) if (i, j) != (0, 0)]

    def xy_to(step):
        return lax.rem(x + step[0], nx), lax.rem(y + step[1], ny)

    def z_to(step):
        return lax.rem(zh + step[0], nh), lax.rem(zl + step[1], nl)

    sibling = (x, zl, y, zh, nc - 1 - co)

    def xy_dev(step):
        tx, ty = xy_to(step)
        return (tx, zl, ty, zh, co)

    def z_dev(step):
        th, tl = z_to(step)
        return (x, tl, y, th, co)

    def send(src, dst, ssem, rsem, dev):
        copy = pltpu.make_async_remote_copy(
            src_ref=src, dst_ref=dst, send_sem=ssem, recv_sem=rsem, device_id=dev, device_id_type=MESH
        )
        copy.start()
        return copy

    kf_copy = pltpu.make_async_copy(kf_ref.at[pl.ds(pl.multiple_of(owner * ROWS, ROWS), ROWS)], kf_s, kf_sem)
    kf_copy.start()

    barrier = pltpu.get_barrier_semaphore()
    partners = [brick(*o) for o in GHOSTS] + [xy_dev(s) for s in xy_steps] + [z_dev(s) for s in z_steps] + [sibling]
    for dev in partners:
        pl.semaphore_signal(barrier, inc=1, device_id=dev, device_id_type=MESH)

    hb = h_ref[...]
    tab_s[...] = jnp.zeros((8, 128), f32)
    tab_s[0:4, 0:CH] = gain_ref[...]
    tab = jnp.transpose(tab_s[...])[0:CH]
    lab = lab_ref[...]
    gains = jnp.zeros((CH, ATOMS), f32)
    for s in range(4):
        gains = jnp.where(lab == s, tab[:, s : s + 1], gains)
    gains_s[...] = gains
    mix = mix_ref[...]
    mix_t = jnp.transpose(mix.astype(f32)).astype(bf16)
    z = (dot_nn(mix_t, hb) * gains).astype(bf16).astype(f32)
    p = pos_ref[...]
    p_hi = p.astype(bf16).astype(f32)
    p_mid = (p - p_hi).astype(bf16).astype(f32)
    p_lo = (p - p_hi - p_mid).astype(bf16).astype(f32)
    rows = jnp.concatenate([z, p_hi, p_mid, p_lo, jnp.zeros((55, ATOMS), f32)], axis=0)
    rows = jnp.transpose(rows).astype(bf16)
    feat[...] = rows[0:432].reshape(3, 3, 3, 16, 128)
    feat5[...] = rows[432:512].reshape(5, 16, 128)

    pl.semaphore_wait(barrier, len(partners))
    ghost_copies = [
        send(pick(feat, o), region(o, gf, ge, gc), gs.at[n], gr.at[n], brick(-o[0], -o[1], -o[2]))
        for n, o in enumerate(GHOSTS)
    ]

    st = jnp.concatenate([hb, dy_ref[...]], axis=0)
    st_s[...] = st
    stt_s[...] = jnp.transpose(st.astype(f32)).astype(bf16)
    mil = mil_ref[...].astype(f32)
    mrows = jnp.concatenate([mil, mil, mil, jnp.zeros((7, mil.shape[1]), f32)], axis=0)
    mi_s[...] = mrows.astype(bf16)
    m9_s[...] = jnp.transpose(mrows).astype(bf16)
    absolute = jnp.concatenate(
        [
            (p[0:1] + x.astype(f32)) * (1.0 / nx),
            (p[1:2] + gy.astype(f32)) * (1.0 / n_gy),
            (p[2:3] + gz.astype(f32)) * (1.0 / n_gz),
        ],
        axis=0,
    )
    w_hi = absolute.astype(bf16).astype(f32)
    w_mid = (absolute - w_hi).astype(bf16).astype(f32)
    w_lo = (absolute - w_hi - w_mid).astype(bf16).astype(f32)
    p9_s[...] = jnp.concatenate([w_hi, w_mid, w_lo, jnp.zeros((7, ATOMS), f32)], axis=0).astype(bf16)

    chunk = 16 if devices >= 16 else devices

    def phase_step(n, _):
        at = pl.multiple_of(n * (chunk * ROWS), chunk * ROWS)
        t = dot_nn(m9_s[pl.ds(at, chunk * ROWS), :], p9_s[...])
        t = t - jnp.floor(t + 0.5)
        sq = t * t
        cosine = poly(COS, sq).reshape(chunk, ROWS, ATOMS)
        sine = (t * poly(SIN, sq)).reshape(chunk, ROWS, ATOMS)
        both = jnp.concatenate([cosine, sine], axis=1).reshape(chunk * 2 * ROWS, ATOMS).astype(bf16)
        cs[pl.ds(pl.multiple_of(n * (chunk * 2 * ROWS), chunk * 2 * ROWS), chunk * 2 * ROWS), :] = both
        part = dot_nn(both, stt_s[...])
        tot[pl.ds(n * (chunk // nc), chunk // nc)] = part.reshape(chunk // nc, nc, 16, 128)
        return 0

    lax.fori_loop(0, devices // chunk, phase_step, 0)

    core_copy = send(tot.at[:, nc - 1 - co], rec_a, cs_s.at[0], cs_r.at[0], sibling)

    e = idx_ref[...]
    slot, atom = e >> 9, e & 511
    block = atom >> 4
    o1 = (slot * 57) >> 9
    o2 = ((slot - 9 * o1) * 11) >> 5
    o3 = slot - 9 * o1 - 3 * o2
    c1 = (block * 57) >> 9
    c2 = ((block - 9 * c1) * 11) >> 5
    c3 = block - 9 * c1 - 3 * c2
    place = jnp.zeros_like(e)
    for o_n, c_n in ((o1, c1), (o2, c2), (o3, c3)):
        place = jnp.where(o_n == 1, place * 3 + c_n, place)
    base = jnp.zeros_like(e)
    for n, o in enumerate(SLOTS):
        base = jnp.where(slot == n, base_block(o), base)
    row = jnp.where(slot == 13, block, base + place) * 16 + (atom & 15)
    segment = jnp.where(row >= 2 * SEG, 2, jnp.where(row >= SEG, 1, 0))
    low = row - SEG * segment
    for j in range(NBR):
        meta[j] = jnp.concatenate(
            [v[j : j + 1] for v in (low, segment, o1 - 1, o2 - 1, o3 - 1)] + [jnp.zeros((3, ATOMS), i32)], axis=0
        )

    core_copy.wait_recv()

    def core_sum(n, _):
        part = tot[pl.ds(n * (nl * ny * nh), nl * ny * nh), co] + rec_a[pl.ds(n * (nl * ny * nh), nl * ny * nh)]
        a_bf[n] = part.astype(bf16).reshape(nl, ny, nh, 16, 128)
        return 0

    lax.fori_loop(0, nx, core_sum, 0)

    xy_copies = []
    for n, s in enumerate(xy_steps):
        tx, ty = xy_to(s)
        xy_copies.append(send(a_bf.at[tx, :, ty], rec_b.at[n], xs.at[n], xr.at[n], xy_dev(s)))

    for c in ghost_copies:
        c.wait_recv()

    table = jnp.concatenate(
        [
            feat[...].reshape(432, 128),
            feat5[...].reshape(80, 128),
            gf[...].reshape(864, 128),
            ge[...].reshape(576, 128),
            gc[...].reshape(128, 128),
            jnp.zeros((224, 128), bf16),
        ],
        axis=0,
    ).astype(f32)
    table = jnp.concatenate(
        [jnp.transpose(table[k * SEG : (k + 1) * SEG])[0:FEAT] for k in range(3)], axis=0
    ).astype(bf16)
    rad = rad_ref[...]
    rad_hi, rad_lo = split2(rad)
    radt_hi, radt_lo = split2(jnp.transpose(rad))
    rad_fwd = jnp.concatenate([radt_hi, radt_hi, radt_lo], axis=1)
    rad_bwd = jnp.concatenate([rad_hi, rad_hi, rad_lo], axis=1)
    spacing = reach_sq / (NB - 1)
    centres = lax.broadcasted_iota(i32, (NB, ATOMS), 0).astype(f32) * spacing
    agg_s[...] = jnp.zeros((CH, ATOMS), f32)

    def forward_step(j, _):
        m = meta[j]
        low_j, seg_j = m[0:1], m[1:2]
        hot = jnp.where(lax.broadcasted_iota(i32, (SEG, ATOMS), 0) == low_j, 1.0, 0.0).astype(bf16)
        onehot[j] = hot
        got = dot_nn(table, hot)
        got = jnp.where(
            seg_j == 0, got[0:FEAT], jnp.where(seg_j == 1, got[FEAT : 2 * FEAT], got[2 * FEAT : 3 * FEAT])
        )
        nz = got[0:CH]
        near[j] = nz.astype(bf16)
        rest = got[CH:FEAT]
        near_pos = (rest[0:3] + rest[3:6]) + rest[6:9]
        rel = (near_pos + m[2:5].astype(f32)) - pos_ref[...]
        sq = rel * rel
        dist = sq[0:1] + sq[1:2] + sq[2:3]
        rel_s[j] = jnp.concatenate([rel, dist, jnp.zeros((4, ATOMS), f32)], axis=0)
        d = (dist - centres) / (2.0 * spacing)
        b = jnp.exp(-(d * d))
        basis_s[j] = b
        b_hi, b_lo = split2(b)
        fl = dot_nn(rad_fwd, jnp.concatenate([b_hi, b_lo, b_hi], axis=0))
        filt[j] = fl
        agg_s[...] += fl * nz
        return 0

    lax.fori_loop(0, NBR, forward_step, 0)

    v = agg_s[...] * NBR ** (-0.5)
    sig = 1.0 / (1.0 + jnp.exp(-v))
    u_s[...] = dy_ref[...].astype(f32) * (sig * (1.0 + v * (1.0 - sig))) * NBR ** (-0.5)

    for c in xy_copies:
        c.wait_recv()
    part = a_bf[x, :, y].astype(f32)
    for n in range(len(xy_steps)):
        part = part + rec_b[n].astype(f32)
    sum_b[...] = part

    z_copies = []
    for n, s in enumerate(z_steps):
        th, tl = z_to(s)
        z_copies.append(send(sum_b.at[tl, th], rec_c.at[n], zs.at[n], zr.at[n], z_dev(s)))

    grad_s[...] = jnp.zeros((SEG, 3 * FEAT), f32)
    ownpos_s[...] = jnp.zeros((8, ATOMS), f32)
    drad_s[...] = jnp.zeros((2 * NB, 2 * CH), f32)

    def backward_step(j, _):
        u = u_s[...]
        nz = near[j].astype(f32)
        dz = u * filt[j]
        df = u * nz
        df_hi, df_lo = split2(df)
        b = basis_s[j]
        b_hi, b_lo = split2(b)
        db = dot_nn(rad_bwd, jnp.concatenate([df_hi, df_lo, df_hi], axis=0))
        drad_s[...] += dot_nt(
            jnp.concatenate([b_hi, b_lo], axis=0), jnp.concatenate([df_hi, df_lo], axis=0)
        )
        r = rel_s[j]
        d = (r[3:4] - centres) / (2.0 * spacing)
        ddist = jnp.sum(db * b * d, axis=0, keepdims=True) * (-2.0 / (2.0 * spacing))
        drel = 2.0 * r[0:3] * ddist
        ownpos_s[0:3] += drel
        drel_hi = drel.astype(bf16).astype(f32)
        stack = jnp.concatenate([dz, drel_hi, drel - drel_hi, jnp.zeros((10, ATOMS), f32)], axis=0)
        seg_j = meta[j][1:2]
        dg = jnp.concatenate([jnp.where(seg_j == k, stack, 0.0) for k in range(3)], axis=0)
        dgs[...] = dg.astype(bf16)
        grad_s[...] += dot_nt(onehot[j], dgs[...])
        return 0

    half = NBR // 2
    lax.fori_loop(0, half, backward_step, 0)

    for c in z_copies:
        c.wait_recv()
    total = sum_b[zl, zh]
    for n in range(len(z_steps)):
        total = total + rec_c[n]
    kf_copy.wait()
    kf = kf_s[...]
    struct = total[:, 0:CH] * norm_atoms
    back = total[:, CH : 2 * CH] * norm_k
    prod = struct * back
    filter_out[...] = prod[0:ROWS] + prod[ROWS : 2 * ROWS]
    kf2 = jnp.concatenate([kf, kf], axis=0)
    coeffs = jnp.concatenate([norm_atoms * kf2 * back, norm_k * kf2 * struct], axis=1).astype(bf16)
    g1[zl, zh] = coeffs
    az_copies = [
        send(g1.at[zl, zh], g1.at[zl, zh], azs.at[n], azr.at[n], z_dev(s)) for n, s in enumerate(z_steps)
    ]

    lax.fori_loop(half, NBR, backward_step, 0)

    grad = grad_s[...]
    table_grad = jnp.concatenate(
        [
            jnp.concatenate([grad[:, k * FEAT : (k + 1) * FEAT], jnp.zeros((SEG, 128 - FEAT), f32)], axis=1)
            for k in range(3)
        ],
        axis=0,
    )
    own_s[...] = table_grad[0:512].reshape(32, 16, 128)
    sf[...] = table_grad[512:1376].astype(bf16).reshape(6, 3, 3, 16, 128)
    se[...] = table_grad[1376:1952].astype(bf16).reshape(12, 3, 16, 128)
    sc[...] = table_grad[1952:2080].astype(bf16).reshape(8, 16, 128)
    back_copies = [
        send(region(o, sf, se, sc), region(o, rf, re, rc), bs.at[n], br.at[n], brick(*o))
        for n, o in enumerate(GHOSTS)
    ]

    for c in az_copies:
        c.wait_recv()
    arr[x, :, y, :, co] = g1[...]
    ax_copies = [
        send(g1, arr.at[x, :, y, :, co], axs.at[n], axr.at[n], xy_dev(s)) for n, s in enumerate(xy_steps)
    ]

    for c in back_copies:
        c.wait_recv()
    for o in GHOSTS:
        got = region(o, rf, re, rc)[...].astype(f32)
        view = [range(3) if c == 0 else [1 - c] for c in o]
        got = got.reshape(-1, 16, 128)
        n = 0
        for i in view[0]:
            for k in view[1]:
                for l in view[2]:
                    own_s[9 * i + 3 * k + l] += got[n]
                    n += 1
    own = jnp.transpose(own_s[...].reshape(512, 128))
    gains = gains_s[...]
    zscaled = (own[0:CH] * gains).astype(bf16)
    pos_short = (own[64:67] + own[67:70]) - ownpos_s[0:3]
    ew_s[...] = dy_ref[...].astype(f32) + dot_nn(mix_ref[...], zscaled)
    weight = dot_nt(h_ref[...], zscaled)
    dr = drad_s[...]
    dr = dr[0:NB, 0:CH] + (dr[NB : 2 * NB, 0:CH] + dr[0:NB, CH : 2 * CH]) + dr[NB : 2 * NB, CH : 2 * CH]
    small = jnp.concatenate(
        [
            jnp.concatenate([weight[0:32], weight[32:64]], axis=1),
            jnp.concatenate([dr[0:8], dr[8:16]], axis=1),
            jnp.zeros((8, 128), f32),
        ],
        axis=0,
    )
    ar_l[...] = small.reshape(2, 24, 128)
    rc_copy = send(ar_l.at[nc - 1 - co], ar_r, rcs.at[0], rcr.at[0], sibling)

    for c in ax_copies:
        c.wait_recv()
    ac_copy = send(
        arr.at[:, :, :, :, co], arr.at[:, :, :, :, co], acs.at[0], acr.at[0], sibling
    )

    rc_copy.wait_recv()
    ar_x[x * ny + y] = ar_l[co] + ar_r[...]
    rx_copies = [
        send(ar_x.at[x * ny + y], ar_x.at[x * ny + y], rxs.at[n], rxr.at[n], xy_dev(s))
        for n, s in enumerate(xy_steps)
    ]
    ac_copy.wait_recv()

    ep_s[...] = jnp.zeros((16, ATOMS), f32)

    def ewald_step(n, _):
        rows_n = chunk * 2 * ROWS
        co_n = arr_chunk(n)
        cs_n = cs[pl.ds(pl.multiple_of(n * rows_n, rows_n), rows_n), :]
        along = dot_nn(co_n, st_s[...]).reshape(chunk, 2, ROWS, ATOMS)
        trig = cs_n.astype(f32).reshape(chunk, 2, ROWS, ATOMS)
        ag = (along[:, 1] * trig[:, 0] - along[:, 0] * trig[:, 1]).reshape(chunk * ROWS, ATOMS)
        ag_hi, ag_lo = split2(ag)
        m_n = mi_s[:, pl.ds(pl.multiple_of(n * (chunk * ROWS), chunk * ROWS), chunk * ROWS)]
        ep_s[...] += dot_nn(m_n, ag_hi) + dot_nn(m_n, ag_lo)
        co_t = jnp.transpose(co_n.astype(f32))[0:CH].astype(bf16)
        ew_s[...] += dot_nn(co_t, cs_n)
        return 0

    per_x = nl * ny * nh * nc // chunk

    def arr_chunk(n):
        i = n // per_x
        r = lax.rem(n, per_x)
        if nl * ny * nh * nc // nl == chunk:
            return arr[i, r].reshape(chunk * 16, 128)
        return arr[i].reshape(chunk * 16, 128)

    steps = devices // chunk
    lax.fori_loop(0, steps // 2, ewald_step, 0)

    for c in rx_copies:
        c.wait_recv()
    part = ar_x[0]
    for n in range(1, nx * ny):
        part = part + ar_x[n]
    ar_z[zl * nh + zh] = part
    rz_copies = [
        send(ar_z.at[zl * nh + zh], ar_z.at[zl * nh + zh], rzs.at[n], rzr.at[n], z_dev(s))
        for n, s in enumerate(z_steps)
    ]

    lax.fori_loop(steps // 2, steps, ewald_step, 0)
    atom_out[...] = ew_s[...].astype(bf16)
    ep = ep_s[0:3]
    turn = 2.0 * math.pi
    pos_out[...] = pos_short + jnp.concatenate(
        [ep[0:1] * (turn / nx), ep[1:2] * (turn / n_gy), ep[2:3] * (turn / n_gz)], axis=0
    )

    for c in rz_copies:
        c.wait_recv()
    part = ar_z[0]
    for n in range(1, nl * nh):
        part = part + ar_z[n]
    ar_o[co] = part
    ro_copy = send(ar_o.at[co], ar_o.at[co], ros.at[0], ror.at[0], sibling)
    ro_copy.wait_recv()
    full = ar_o[...].reshape(48, 128)
    weight_out[...] = jnp.concatenate([full[0:32, 0:CH], full[0:32, CH : 2 * CH]], axis=0)
    radial_out[...] = jnp.concatenate([full[32:40, 0:CH], full[32:40, CH : 2 * CH]], axis=0)

    for c in (
        ghost_copies + [core_copy] + xy_copies + z_copies + az_copies + ax_copies + back_copies
        + [rc_copy, ac_copy] + rx_copies + rz_copies + [ro_copy]
    ):
        c.wait_send()


def shards(sizes, h, dy, pos, labels, entries, miller, kfilter, mix, table, radial):
    nx, nl, ny, nh, nc = sizes
    devices = nx * nl * ny * nh * nc
    k = ROWS * devices
    nxy, nz = nx * ny, nl * nh
    vmem = pl.BlockSpec(memory_space=pltpu.VMEM)
    dma = pltpu.SemaphoreType.DMA
    plane = devices // nc
    scratch = [
        pltpu.VMEM((2 * k, ATOMS), bf16),
        pltpu.VMEM((plane, nc, 16, 128), f32),
        pltpu.VMEM((nx, nl, ny, nh, nc, 16, 128), bf16),
        pltpu.VMEM((3, 3, 3, 16, 128), bf16),
        pltpu.VMEM((5, 16, 128), bf16),
        pltpu.VMEM((6, 3, 3, 16, 128), bf16),
        pltpu.VMEM((12, 3, 16, 128), bf16),
        pltpu.VMEM((8, 16, 128), bf16),
        pltpu.VMEM((NBR, 8, ATOMS), i32),
        pltpu.VMEM((NBR, SEG, ATOMS), bf16),
        pltpu.VMEM((NBR, CH, ATOMS), bf16),
        pltpu.VMEM((NBR, CH, ATOMS), f32),
        pltpu.VMEM((NBR, NB, ATOMS), f32),
        pltpu.VMEM((NBR, 8, ATOMS), f32),
        pltpu.VMEM((3 * FEAT, ATOMS), bf16),
        pltpu.VMEM((CH, ATOMS), f32),
        pltpu.VMEM((SEG, 3 * FEAT), f32),
        pltpu.VMEM((32, 16, 128), f32),
        pltpu.VMEM((8, ATOMS), f32),
        pltpu.VMEM((CH, ATOMS), f32),
        pltpu.VMEM((2 * NB, 2 * CH), f32),
        pltpu.VMEM((6, 3, 3, 16, 128), bf16),
        pltpu.VMEM((12, 3, 16, 128), bf16),
        pltpu.VMEM((8, 16, 128), bf16),
        pltpu.VMEM((6, 3, 3, 16, 128), bf16),
        pltpu.VMEM((12, 3, 16, 128), bf16),
        pltpu.VMEM((8, 16, 128), bf16),
        pltpu.VMEM((plane, 16, 128), f32),
        pltpu.VMEM((nx, nl, ny, nh, 16, 128), bf16),
        pltpu.VMEM((nxy - 1, nl, nh, 16, 128), bf16),
        pltpu.VMEM((nl, nh, 16, 128), f32),
        pltpu.VMEM((nz - 1, 16, 128), f32),
        pltpu.VMEM((nl, nh, 16, 128), bf16),
        pltpu.VMEM((k, 16), bf16),
        pltpu.VMEM((16, ATOMS), bf16),
        pltpu.VMEM((2 * CH, ATOMS), bf16),
        pltpu.VMEM((ATOMS, 2 * CH), bf16),
        pltpu.VMEM((CH, ATOMS), f32),
        pltpu.VMEM((CH, ATOMS), f32),
        pltpu.VMEM((16, ATOMS), f32),
        pltpu.VMEM((ROWS, CH), f32),
        pltpu.VMEM((16, k), bf16),
        pltpu.VMEM((8, 128), f32),
        pltpu.VMEM((2, 24, 128), f32),
        pltpu.VMEM((24, 128), f32),
        pltpu.VMEM((nxy, 24, 128), f32),
        pltpu.VMEM((nz, 24, 128), f32),
        pltpu.VMEM((2, 24, 128), f32),
        dma,
    ]
    for count in (26, 26, 1, nxy - 1, nz - 1, nz - 1, nxy - 1, 1, 1, nxy - 1, nz - 1, 1):
        scratch += [dma((count,)), dma((count,))]
    out = pl.pallas_call(
        functools.partial(kernel, sizes),
        out_shape=(
            jax.ShapeDtypeStruct((CH, ATOMS), bf16),
            jax.ShapeDtypeStruct((3, ATOMS), f32),
            jax.ShapeDtypeStruct((CH, CH), f32),
            jax.ShapeDtypeStruct((NB, CH), f32),
            jax.ShapeDtypeStruct((ROWS, CH), f32),
        ),
        in_specs=[vmem] * 6 + [pl.BlockSpec(memory_space=pl.ANY)] + [vmem] * 3,
        out_specs=(vmem,) * 5,
        scratch_shapes=scratch,
        compiler_params=pltpu.CompilerParams(
            collective_id=0, has_side_effects=True, vmem_limit_bytes=60 * 1024 * 1024
        ),
        name="layer",
    )(
        h[0, 0, 0], dy[0, 0, 0], pos[0, 0, 0], labels[0, 0], entries[0, 0, 0],
        miller, kfilter, mix, table, radial,
    )
    return (out[0][None, None, None], out[1][None, None, None], out[2], out[3], out[4])


def solution(mesh):
    sizes = (mesh.shape["gx"], 4, mesh.shape["gy"] // 4, mesh.shape["gz"] // 2, 2)
    finer = Mesh(mesh.devices.reshape(sizes), AXES)
    brick = P("gx", GY, GZ, None, None)
    return jax.shard_map(
        functools.partial(shards, sizes),
        mesh=finer,
        in_specs=(brick, brick, brick, P("gx", GY, GZ, None), brick, P(), P(), P(), P(), P()),
        out_specs=(brick, brick, P(), P(), P(AXES, None)),
        check_vma=False,
    )
```

time: 464 us -> 80.6 us (0.17)
  other arithmetic: 142 us -> 0 us
  local copies, waits for them, and re-layouts: 103 us -> 8.39 us
  Pallas kernels: 0 us -> 71.2 us
  blocking collectives: 71 us -> 0 us
  matrix products: 53.5 us -> 0 us
  starting transfers between devices: 52.6 us -> 0 us
  waiting for transfers between devices: 23 us -> 0 us
  between operations: 15 us -> 0.66 us
    scatter-add x2 -> x0, other arithmetic: 95.4 us -> none  [the longest x1 47.7 us: short_range(): near_z = flat_z[:, neighbour_ids]]
    pallas_call x0 -> x1, Pallas kernels: none -> 71.2 us  [shards(): pl.pallas_call(functools.partial(kernel, sizes), out_shape=(jax.ShapeDtyp...]
    psum x5 -> x0, blocking collectives: 71 us -> none  [by_axis(): return functools.reduce(lax.psum, axes, x)]
    gather x3 -> x0, local copies, waits for them, and re-layouts: 67 us -> none  [the longest x2 36.3 us: short_range(): near_z = flat_z[:, neighbour_ids]]
    dot_general x29 -> x0, matrix products: 53.5 us -> none  [the longest x1 15.4 us: structure_terms(): lax.dot_general(cos_part, stacked, contract, preferred_element_type=jnp.f...]
    ppermute x24 -> x0, starting transfers between devices: 52.6 us -> none  [the longest x12 25.3 us: from_behind(): lax.ppermute(x, axis, [(i, (i + by) % devices) for i in range(devices)])]
    ppermute x24 -> x0, waiting for transfers between devices: 23 us -> none  [the longest x6 10.1 us: padded(): before = lax.ppermute(last, axis, up)]
    convert_element_type x3 -> x0, other arithmetic: 17.1 us -> none  [the longest x1 17 us: phases(): jnp.sin(angles).astype(jnp.bfloat16)]
  transfers between devices with their start and end apart: 25 -> 0, of which waited for: 7 -> 0; matrix products, arithmetic and copies ran while one was open for 64% -> 0% of each run, Pallas kernels for 0% -> 0%
where the time goes in v1:
time: 80.6 us; the launch traced here: 80.2 us
  Pallas kernels  71.2 us (88%)
  local copies, waits for them, and re-layouts  8.39 us (10%)
    pallas_call x1, Pallas kernels, shards(): pl.pallas_call(functools.partial(kernel, sizes), out_shape=(jax.ShapeDtyp...  71.2 us
    unnamed x17, local copies, waits for them, and re-layouts  8.39 us

profile of v1, /device:TPU:1, one launch (start us, length us, event | category | flops | bytes accessed | tf_op | source)
XLA Modules:
  0.0 80.2 jit_solution(15816706652657310838)
XLA Ops:
  0.6 0.0 copy-start.3
  0.6 0.7 copy-done.3
  1.3 0.6 copy.19
  1.9 2.4 %copy.15.kf_ref = f32[2048,64]{1,0:T(8,128)} copy(f32[2048,64]{0,1:T(8,128)} %param.16) | data formatting | bytes 1048576 | tf_op args[6]
  4.3 71.2 %layer.1 = (bf16[64,512]{1,0:T(8,128)(2,1)}, f32[3,512]{1,0:T(4,128)}, f32[64,64]{1,0:T(8,128)}, f32[16,64]{1,0:T(8,128)}, f32[8,64]{1,0:T(8,128)}) custom-call(bf16[64,512]{1,0:T(8,128)(2,1)} %bitcast.9, bf16[64,512]{1,0:T(8,128)(2,1)} %bitcast.10, f32[3,512]{1,0:T(4,128)} %bitcast.12, s32[1,512]{1,0:T(1,128)} %bitcast.15, s32[16,512]{1,0:T(8,128)} %bitcast.13, ...), custom_call_target="tpu_custom_call" | custom-call | tf_op jit(solution)/shard_map/layer/pallas_call | solution.py:579
  75.4 0.0 copy-start.1
  75.5 0.7 copy-done.1
  76.1 0.6 copy.16
  76.7 0.0 copy-start
  76.7 1.5 %copy.24 = bf16[1,1,1,64,512]{4,3,2,1,0:T(8,128)(2,1)} copy(bf16[1,1,1,64,512]{4,3,2,1,0:T(8,128)(2,1)} %bitcast.11) | data formatting | bytes 131072
  78.2 0.0 copy-done
  78.2 0.0 copy-start.2
  78.2 0.6 copy.25
  78.8 0.1 copy-done.2
  78.9 0.0 copy-start.4
  78.9 0.6 copy.26
  79.5 0.1 copy-done.4
  79.6 0.6 copy.27
Async XLA Ops:
  0.6 0.7 copy-start.3
  75.4 0.7 copy-start.1
  76.7 1.5 %copy-start = (f32[64,64]{1,0:T(8,128)S(1)}, f32[64,64]{1,0:T(8,128)}, u32[]{:S(2)}) copy-start(f32[64,64]{1,0:T(8,128)} %get-tuple-element.27) | copy-start | bytes 49156
  78.2 0.7 copy-start.2
  78.9 0.7 copy-start.4

commit v2 on v1

--- a/solution.py
+++ b/solution.py
@@ -20,8 +20,9 @@
 NBR = 16
 NB = 16
 ROWS = 8
-SEG = 768
-FEAT = 80
+SEG = 528
+BLOCKS = 144
+GROUP = 4
 reach_sq = 0.75
 
 COS = (
@@ -72,6 +73,13 @@
     return hi, (x - hi.astype(f32)).astype(bf16)
 
 
+def split3(x):
+    hi = x.astype(bf16)
+    rest = x - hi.astype(f32)
+    mid = rest.astype(bf16)
+    return hi, mid, (rest - mid.astype(f32)).astype(bf16)
+
+
 def dot_nn(a, b):
     return jnp.dot(a, b, preferred_element_type=f32)
 
@@ -98,10 +106,11 @@
     atom_out, pos_out, weight_out, radial_out, filter_out,
     cs, tot, arr,
     feat, feat5, gf, ge, gc,
+    pfeat, pfeat5, pgf, pge, pgc, psf, pse, psc, prf, pre, prc, table_s, xp_s, hotb, dgp, gradp_s, ownp_s,
     meta, onehot, near, filt, basis_s, rel_s, dgs, agg_s, grad_s, own_s, ownpos_s, u_s, drad_s,
     sf, se, sc, rf, re, rc,
     rec_a, a_bf, rec_b, sum_b, rec_c, g1,
-    m9_s, p9_s, st_s, stt_s, gains_s, ew_s, ep_s, kf_s, mi_s, tab_s,
+    m9_s, p9_s, st_s, stt_s, gains_s, ew_s, ep_s, kf_s, kft_s, mi_s, tab_s, pos_s,
     ar_l, ar_r, ar_x, ar_z, ar_o,
     kf_sem, gs, gr, bs, br, cs_s, cs_r, xs, xr, zs, zr, azs, azr, axs, axr, acs, acr,
     rcs, rcr, rxs, rxr, rzs, rzr, ros, ror,
@@ -147,7 +156,7 @@
         copy.start()
         return copy
 
-    kf_copy = pltpu.make_async_copy(kf_ref.at[pl.ds(pl.multiple_of(owner * ROWS, ROWS), ROWS)], kf_s, kf_sem)
+    kf_copy = pltpu.make_async_copy(kf_ref.at[:, pl.ds(pl.multiple_of(owner // 16 * 128, 128), 128)], kf_s, kf_sem)
     kf_copy.start()
 
     barrier = pltpu.get_barrier_semaphore()
@@ -166,21 +175,23 @@
     gains_s[...] = gains
     mix = mix_ref[...]
     mix_t = jnp.transpose(mix.astype(f32)).astype(bf16)
-    z = (dot_nn(mix_t, hb) * gains).astype(bf16).astype(f32)
-    p = pos_ref[...]
-    p_hi = p.astype(bf16).astype(f32)
-    p_mid = (p - p_hi).astype(bf16).astype(f32)
-    p_lo = (p - p_hi - p_mid).astype(bf16).astype(f32)
-    rows = jnp.concatenate([z, p_hi, p_mid, p_lo, jnp.zeros((55, ATOMS), f32)], axis=0)
-    rows = jnp.transpose(rows).astype(bf16)
-    feat[...] = rows[0:432].reshape(3, 3, 3, 16, 128)
-    feat5[...] = rows[432:512].reshape(5, 16, 128)
-
-    pl.semaphore_wait(barrier, len(partners))
-    ghost_copies = [
-        send(pick(feat, o), region(o, gf, ge, gc), gs.at[n], gr.at[n], brick(-o[0], -o[1], -o[2]))
-        for n, o in enumerate(GHOSTS)
-    ]
+    z = jnp.transpose((dot_nn(mix_t, hb) * gains).astype(bf16).astype(f32)).reshape(32, 2, 8, CH)
+    z = jnp.concatenate([z[:, 0], z[:, 1]], axis=2).astype(bf16)
+    feat[...] = z[0:27].reshape(3, 3, 3, 8, 128)
+    feat5[...] = z[27:32]
+    p = pos_ref[:, 0, :]
+    pos_s[...] = p
+    lane = lax.broadcasted_iota(i32, (16, ATOMS), 1)
+    in_block = (lane & 15) == lax.broadcasted_iota(i32, (16, ATOMS), 0)
+    block_hot = jnp.where(
+        lax.broadcasted_iota(i32, (32, ATOMS), 1) >> 4 == lax.broadcasted_iota(i32, (32, ATOMS), 0), 1.0, 0.0
+    ).astype(bf16)
+    spread = jnp.concatenate([jnp.where(in_block, p[d : d + 1], 0.0) for d in range(3)], axis=0)
+    parts = dot_nt(jnp.concatenate(split3(spread), axis=0), block_hot)
+    parts = (parts[0:48] + parts[48:96]) + parts[96:144]
+    parts = jnp.transpose(jnp.concatenate([parts, jnp.zeros((80, 32), f32)], axis=0))
+    pfeat[...] = parts[0:27].reshape(3, 3, 3, 1, 128)
+    pfeat5[...] = parts[27:32].reshape(5, 1, 128)
 
     st = jnp.concatenate([hb, dy_ref[...]], axis=0)
     st_s[...] = st
@@ -219,7 +230,16 @@
 
     lax.fori_loop(0, devices // chunk, phase_step, 0)
 
+    pl.semaphore_wait(barrier, len(partners))
     core_copy = send(tot.at[:, nc - 1 - co], rec_a, cs_s.at[0], cs_r.at[0], sibling)
+
+    ghost_copies = [
+        send(pick(feat, o), region(o, gf, ge, gc), gs.at[n], gr.at[n], brick(-o[0], -o[1], -o[2]))
+        for n, o in enumerate(GHOSTS)
+    ] + [
+        send(pick(pfeat, o), region(o, pgf, pge, pgc), gs.at[26 + n], gr.at[26 + n], brick(-o[0], -o[1], -o[2]))
+        for n, o in enumerate(GHOSTS)
+    ]
 
     e = idx_ref[...]
     slot, atom = e >> 9, e & 511
@@ -236,12 +256,17 @@
     base = jnp.zeros_like(e)
     for n, o in enumerate(SLOTS):
         base = jnp.where(slot == n, base_block(o), base)
-    row = jnp.where(slot == 13, block, base + place) * 16 + (atom & 15)
-    segment = jnp.where(row >= 2 * SEG, 2, jnp.where(row >= SEG, 1, 0))
-    low = row - SEG * segment
+    at_block = jnp.where(slot == 13, block, base + place)
+    inner = atom & 15
+    row = at_block * 8 + (inner & 7)
+    upper = jnp.where(row >= 512, 1, 0)
+    low = row - 512 * upper
+    segment = 2 * upper + (inner >> 3)
     for j in range(NBR):
         meta[j] = jnp.concatenate(
-            [v[j : j + 1] for v in (low, segment, o1 - 1, o2 - 1, o3 - 1)] + [jnp.zeros((3, ATOMS), i32)], axis=0
+            [v[j : j + 1] for v in (low, segment, at_block, inner, o1 - 1, o2 - 1, o3 - 1)]
+            + [jnp.zeros((1, ATOMS), i32)],
+            axis=0,
         )
 
     core_copy.wait_recv()
@@ -258,23 +283,48 @@
         tx, ty = xy_to(s)
         xy_copies.append(send(a_bf.at[tx, :, ty], rec_b.at[n], xs.at[n], xr.at[n], xy_dev(s)))
 
+    def hot_step(n, _):
+        for k in range(GROUP):
+            m = meta[n * GROUP + k]
+            at = slice(k * ATOMS, (k + 1) * ATOMS)
+            onehot[n, :, at] = jnp.where(
+                lax.broadcasted_iota(i32, (SEG, ATOMS), 0) == m[0:1], 1.0, 0.0
+            ).astype(bf16)
+            hotb[n, :, at] = jnp.where(
+                lax.broadcasted_iota(i32, (BLOCKS, ATOMS), 0) == m[2:3], 1.0, 0.0
+            ).astype(bf16)
+        return 0
+
+    lax.fori_loop(0, NBR // GROUP, hot_step, 0)
+
     for c in ghost_copies:
         c.wait_recv()
 
     table = jnp.concatenate(
         [
-            feat[...].reshape(432, 128),
-            feat5[...].reshape(80, 128),
-            gf[...].reshape(864, 128),
-            ge[...].reshape(576, 128),
-            gc[...].reshape(128, 128),
-            jnp.zeros((224, 128), bf16),
+            feat[...].reshape(216, 128),
+            feat5[...].reshape(40, 128),
+            gf[...].reshape(432, 128),
+            ge[...].reshape(288, 128),
+            gc[...].reshape(64, 128),
         ],
         axis=0,
     ).astype(f32)
     table = jnp.concatenate(
-        [jnp.transpose(table[k * SEG : (k + 1) * SEG])[0:FEAT] for k in range(3)], axis=0
-    ).astype(bf16)
+        [
+            jnp.concatenate([jnp.transpose(table[0:512]), jnp.zeros((128, SEG - 512), f32)], axis=1),
+            jnp.transpose(table[512:1040]),
+        ],
+        axis=0,
+    )
+    table_s[...] = table.astype(bf16)
+    xp_s[...] = jnp.zeros((BLOCKS, 128), f32)
+    xp_s[0:27] = pfeat[...].reshape(27, 128)
+    xp_s[27:32] = pfeat5[...].reshape(5, 128)
+    xp_s[32:86] = pgf[...].reshape(54, 128)
+    xp_s[86:122] = pge[...].reshape(36, 128)
+    xp_s[122:130] = pgc[...].reshape(8, 128)
+    ptable = jnp.concatenate(split3(jnp.transpose(xp_s[...])[0:48]), axis=0)
     rad = rad_ref[...]
     rad_hi, rad_lo = split2(rad)
     radt_hi, radt_lo = split2(jnp.transpose(rad))
@@ -284,20 +334,29 @@
     centres = lax.broadcasted_iota(i32, (NB, ATOMS), 0).astype(f32) * spacing
     agg_s[...] = jnp.zeros((CH, ATOMS), f32)
 
-    def forward_step(j, _):
+    def forward_one(n, k):
+        j = n * GROUP + k
         m = meta[j]
-        low_j, seg_j = m[0:1], m[1:2]
-        hot = jnp.where(lax.broadcasted_iota(i32, (SEG, ATOMS), 0) == low_j, 1.0, 0.0).astype(bf16)
-        onehot[j] = hot
-        got = dot_nn(table, hot)
-        got = jnp.where(
-            seg_j == 0, got[0:FEAT], jnp.where(seg_j == 1, got[FEAT : 2 * FEAT], got[2 * FEAT : 3 * FEAT])
+        seg_j = m[1:2]
+        at = slice(k * ATOMS, (k + 1) * ATOMS)
+        got = dot_nn(table_s[...], onehot[n, :, at])
+        nz = jnp.where(
+            seg_j < 2,
+            jnp.where(seg_j == 0, got[0:CH], got[CH : 2 * CH]),
+            jnp.where(seg_j == 2, got[2 * CH : 3 * CH], got[3 * CH : 4 * CH]),
         )
-        nz = got[0:CH]
         near[j] = nz.astype(bf16)
-        rest = got[CH:FEAT]
-        near_pos = (rest[0:3] + rest[3:6]) + rest[6:9]
-        rel = (near_pos + m[2:5].astype(f32)) - pos_ref[...]
+        gotp = dot_nn(ptable, hotb[n, :, at])
+        gotp = (gotp[0:48] + gotp[48:96]) + gotp[96:144]
+        mine = lax.broadcasted_iota(i32, (16, ATOMS), 0) == m[3:4]
+        near_pos = jnp.concatenate(
+            [
+                jnp.sum(jnp.where(mine, gotp[16 * d : 16 * d + 16], 0.0), axis=0, keepdims=True)
+                for d in range(3)
+            ],
+            axis=0,
+        )
+        rel = (near_pos + m[4:7].astype(f32)) - pos_s[...]
         sq = rel * rel
         dist = sq[0:1] + sq[1:2] + sq[2:3]
         rel_s[j] = jnp.concatenate([rel, dist, jnp.zeros((4, ATOMS), f32)], axis=0)
@@ -307,32 +366,25 @@
         b_hi, b_lo = split2(b)
         fl = dot_nn(rad_fwd, jnp.concatenate([b_hi, b_lo, b_hi], axis=0))
         filt[j] = fl
-        agg_s[...] += fl * nz
+        return fl * nz
+
+    def forward_step(n, _):
+        parts = [forward_one(n, k) for k in range(GROUP)]
+        agg_s[...] += functools.reduce(jnp.add, parts)
         return 0
 
-    lax.fori_loop(0, NBR, forward_step, 0)
+    lax.fori_loop(0, NBR // GROUP, forward_step, 0)
 
     v = agg_s[...] * NBR ** (-0.5)
     sig = 1.0 / (1.0 + jnp.exp(-v))
     u_s[...] = dy_ref[...].astype(f32) * (sig * (1.0 + v * (1.0 - sig))) * NBR ** (-0.5)
 
-    for c in xy_copies:
-        c.wait_recv()
-    part = a_bf[x, :, y].astype(f32)
-    for n in range(len(xy_steps)):
-        part = part + rec_b[n].astype(f32)
-    sum_b[...] = part
-
-    z_copies = []
-    for n, s in enumerate(z_steps):
-        th, tl = z_to(s)
-        z_copies.append(send(sum_b.at[tl, th], rec_c.at[n], zs.at[n], zr.at[n], z_dev(s)))
-
-    grad_s[...] = jnp.zeros((SEG, 3 * FEAT), f32)
+    grad_s[...] = jnp.zeros((SEG, 4 * CH), f32)
+    gradp_s[...] = jnp.zeros((BLOCKS, 96), f32)
     ownpos_s[...] = jnp.zeros((8, ATOMS), f32)
     drad_s[...] = jnp.zeros((2 * NB, 2 * CH), f32)
 
-    def backward_step(j, _):
+    def backward_one(j, k):
         u = u_s[...]
         nz = near[j].astype(f32)
         dz = u * filt[j]
@@ -341,24 +393,66 @@
         b = basis_s[j]
         b_hi, b_lo = split2(b)
         db = dot_nn(rad_bwd, jnp.concatenate([df_hi, df_lo, df_hi], axis=0))
-        drad_s[...] += dot_nt(
-            jnp.concatenate([b_hi, b_lo], axis=0), jnp.concatenate([df_hi, df_lo], axis=0)
-        )
+        drad = dot_nt(jnp.concatenate([b_hi, b_lo], axis=0), jnp.concatenate([df_hi, df_lo], axis=0))
         r = rel_s[j]
         d = (r[3:4] - centres) / (2.0 * spacing)
         ddist = jnp.sum(db * b * d, axis=0, keepdims=True) * (-2.0 / (2.0 * spacing))
         drel = 2.0 * r[0:3] * ddist
-        ownpos_s[0:3] += drel
+        m = meta[j]
+        seg_j = m[1:2]
+        at = slice(k * ATOMS, (k + 1) * ATOMS)
+        dgs[:, at] = jnp.concatenate([jnp.where(seg_j == q, dz, 0.0) for q in range(4)], axis=0).astype(bf16)
         drel_hi = drel.astype(bf16).astype(f32)
-        stack = jnp.concatenate([dz, drel_hi, drel - drel_hi, jnp.zeros((10, ATOMS), f32)], axis=0)
-        seg_j = meta[j][1:2]
-        dg = jnp.concatenate([jnp.where(seg_j == k, stack, 0.0) for k in range(3)], axis=0)
-        dgs[...] = dg.astype(bf16)
-        grad_s[...] += dot_nt(onehot[j], dgs[...])
+        mine = lax.broadcasted_iota(i32, (16, ATOMS), 0) == m[3:4]
+        dgp[:, at] = jnp.concatenate(
+            [jnp.where(mine, v[d : d + 1], 0.0) for v in (drel_hi, drel - drel_hi) for d in range(3)], axis=0
+        ).astype(bf16)
+        return drad, drel
+
+    def backward_step(n, _):
+        parts = [backward_one(n * GROUP + k, k) for k in range(GROUP)]
+        drad_s[...] += functools.reduce(jnp.add, [p[0] for p in parts])
+        ownpos_s[0:3] += functools.reduce(jnp.add, [p[1] for p in parts])
+        grad_s[...] += dot_nt(onehot[n], dgs[...])
+        gradp_s[...] += dot_nt(hotb[n], dgp[...])
         return 0
 
-    half = NBR // 2
+    half = NBR // GROUP // 2
     lax.fori_loop(0, half, backward_step, 0)
+
+    for c in xy_copies:
+        c.wait_recv()
+    part = a_bf[x, :, y].astype(f32)
+    for n in range(len(xy_steps)):
+        part = part + rec_b[n].astype(f32)
+    sum_b[...] = part
+
+    z_copies = []
+    for n, s in enumerate(z_steps):
+        th, tl = z_to(s)
+        z_copies.append(send(sum_b.at[tl, th], rec_c.at[n], zs.at[n], zr.at[n], z_dev(s)))
+
+    lax.fori_loop(half, NBR // GROUP, backward_step, 0)
+
+    grad = grad_s[...]
+    grad = jnp.concatenate([grad[0:512, 0:128], grad[:, 128:256]], axis=0)
+    own_s[...] = grad[0:256].reshape(32, 8, 128)
+    sf[...] = grad[256:688].astype(bf16).reshape(6, 3, 3, 8, 128)
+    se[...] = grad[688:976].astype(bf16).reshape(12, 3, 8, 128)
+    sc[...] = grad[976:1040].astype(bf16).reshape(8, 8, 128)
+    gradp = gradp_s[...]
+    gradp = jnp.concatenate([gradp[:, 0:48] + gradp[:, 48:96], jnp.zeros((BLOCKS, 80), f32)], axis=1)
+    ownp_s[...] = gradp[0:32].reshape(32, 1, 128)
+    psf[...] = gradp[32:86].reshape(6, 3, 3, 1, 128)
+    pse[...] = gradp[86:122].reshape(12, 3, 1, 128)
+    psc[...] = gradp[122:130].reshape(8, 1, 128)
+    back_copies = [
+        send(region(o, sf, se, sc), region(o, rf, re, rc), bs.at[n], br.at[n], brick(*o))
+        for n, o in enumerate(GHOSTS)
+    ] + [
+        send(region(o, psf, pse, psc), region(o, prf, pre, prc), bs.at[26 + n], br.at[26 + n], brick(*o))
+        for n, o in enumerate(GHOSTS)
+    ]
 
     for c in z_copies:
         c.wait_recv()
@@ -366,7 +460,8 @@
     for n in range(len(z_steps)):
         total = total + rec_c[n]
     kf_copy.wait()
-    kf = kf_s[...]
+    kft_s[...] = jnp.transpose(kf_s[...])
+    kf = kft_s[pl.ds(pl.multiple_of(lax.rem(owner, 16) * ROWS, ROWS), ROWS), :]
     struct = total[:, 0:CH] * norm_atoms
     back = total[:, CH : 2 * CH] * norm_k
     prod = struct * back
@@ -378,25 +473,6 @@
         send(g1.at[zl, zh], g1.at[zl, zh], azs.at[n], azr.at[n], z_dev(s)) for n, s in enumerate(z_steps)
     ]
 
-    lax.fori_loop(half, NBR, backward_step, 0)
-
-    grad = grad_s[...]
-    table_grad = jnp.concatenate(
-        [
-            jnp.concatenate([grad[:, k * FEAT : (k + 1) * FEAT], jnp.zeros((SEG, 128 - FEAT), f32)], axis=1)
-            for k in range(3)
-        ],
-        axis=0,
-    )
-    own_s[...] = table_grad[0:512].reshape(32, 16, 128)
-    sf[...] = table_grad[512:1376].astype(bf16).reshape(6, 3, 3, 16, 128)
-    se[...] = table_grad[1376:1952].astype(bf16).reshape(12, 3, 16, 128)
-    sc[...] = table_grad[1952:2080].astype(bf16).reshape(8, 16, 128)
-    back_copies = [
-        send(region(o, sf, se, sc), region(o, rf, re, rc), bs.at[n], br.at[n], brick(*o))
-        for n, o in enumerate(GHOSTS)
-    ]
-
     for c in az_copies:
         c.wait_recv()
     arr[x, :, y, :, co] = g1[...]
@@ -409,17 +485,30 @@
     for o in GHOSTS:
         got = region(o, rf, re, rc)[...].astype(f32)
         view = [range(3) if c == 0 else [1 - c] for c in o]
-        got = got.reshape(-1, 16, 128)
+        got = got.reshape(-1, 8, 128)
+        gotp = region(o, prf, pre, prc)[...].reshape(-1, 1, 128)
         n = 0
         for i in view[0]:
             for k in view[1]:
                 for l in view[2]:
                     own_s[9 * i + 3 * k + l] += got[n]
+                    ownp_s[9 * i + 3 * k + l] += gotp[n]
                     n += 1
-    own = jnp.transpose(own_s[...].reshape(512, 128))
+    own = own_s[...]
+    own = jnp.concatenate([own[:, None, :, 0:CH], own[:, None, :, CH : 2 * CH]], axis=1)
+    own = jnp.transpose(own.reshape(ATOMS, CH))
+    ownp = jnp.transpose(ownp_s[...].reshape(32, 128))[0:48]
+    wide = dot_nn(jnp.concatenate(split3(ownp), axis=1), jnp.concatenate([block_hot] * 3, axis=0))
+    ownp = jnp.concatenate(
+        [
+            jnp.sum(jnp.where(in_block, wide[16 * d : 16 * d + 16], 0.0), axis=0, keepdims=True)
+            for d in range(3)
+        ],
+        axis=0,
+    )
     gains = gains_s[...]
-    zscaled = (own[0:CH] * gains).astype(bf16)
-    pos_short = (own[64:67] + own[67:70]) - ownpos_s[0:3]
+    zscaled = (own * gains).astype(bf16)
+    pos_short = ownp - ownpos_s[0:3]
     ew_s[...] = dy_ref[...].astype(f32) + dot_nn(mix_ref[...], zscaled)
     weight = dot_nt(h_ref[...], zscaled)
     dr = drad_s[...]
@@ -435,17 +524,27 @@
     ar_l[...] = small.reshape(2, 24, 128)
     rc_copy = send(ar_l.at[nc - 1 - co], ar_r, rcs.at[0], rcr.at[0], sibling)
 
+    rc_copy.wait_recv()
+    ar_x[x * ny + y] = ar_l[co] + ar_r[...]
+    rx_copies = [
+        send(ar_x.at[x * ny + y], ar_x.at[x * ny + y], rxs.at[n], rxr.at[n], xy_dev(s))
+        for n, s in enumerate(xy_steps)
+    ]
+
     for c in ax_copies:
         c.wait_recv()
     ac_copy = send(
         arr.at[:, :, :, :, co], arr.at[:, :, :, :, co], acs.at[0], acr.at[0], sibling
     )
-
-    rc_copy.wait_recv()
-    ar_x[x * ny + y] = ar_l[co] + ar_r[...]
-    rx_copies = [
-        send(ar_x.at[x * ny + y], ar_x.at[x * ny + y], rxs.at[n], rxr.at[n], xy_dev(s))
-        for n, s in enumerate(xy_steps)
+    for c in rx_copies:
+        c.wait_recv()
+    part = ar_x[0]
+    for n in range(1, nx * ny):
+        part = part + ar_x[n]
+    ar_z[zl * nh + zh] = part
+    rz_copies = [
+        send(ar_z.at[zl * nh + zh], ar_z.at[zl * nh + zh], rzs.at[n], rzr.at[n], z_dev(s))
+        for n, s in enumerate(z_steps)
     ]
     ac_copy.wait_recv()
 
@@ -475,24 +574,11 @@
         return arr[i].reshape(chunk * 16, 128)
 
     steps = devices // chunk
-    lax.fori_loop(0, steps // 2, ewald_step, 0)
-
-    for c in rx_copies:
-        c.wait_recv()
-    part = ar_x[0]
-    for n in range(1, nx * ny):
-        part = part + ar_x[n]
-    ar_z[zl * nh + zh] = part
-    rz_copies = [
-        send(ar_z.at[zl * nh + zh], ar_z.at[zl * nh + zh], rzs.at[n], rzr.at[n], z_dev(s))
-        for n, s in enumerate(z_steps)
-    ]
-
-    lax.fori_loop(steps // 2, steps, ewald_step, 0)
+    lax.fori_loop(0, steps, ewald_step, 0)
     atom_out[...] = ew_s[...].astype(bf16)
     ep = ep_s[0:3]
     turn = 2.0 * math.pi
-    pos_out[...] = pos_short + jnp.concatenate(
+    pos_out[:, 0, :] = pos_short + jnp.concatenate(
         [ep[0:1] * (turn / nx), ep[1:2] * (turn / n_gy), ep[2:3] * (turn / n_gz)], axis=0
     )
 
@@ -513,6 +599,30 @@
         + [rc_copy, ac_copy] + rx_copies + rz_copies + [ro_copy]
     ):
         c.wait_send()
+
+
+def deliver_kernel(*refs):
+    n = (len(refs) - 1) // 3
+    copies = [pltpu.make_async_copy(refs[i], refs[2 * n + i], refs[-1].at[i]) for i in range(n)]
+    for c in copies:
+        c.start()
+    for c in copies:
+        c.wait()
+    for i in range(n):
+        refs[n + i][...] = refs[2 * n + i][...]
+
+
+def deliver(arrays):
+    return pl.pallas_call(
+        deliver_kernel,
+        out_shape=tuple(jax.ShapeDtypeStruct(a.shape, a.dtype) for a in arrays),
+        in_specs=[pl.BlockSpec(memory_space=pl.ANY)] * len(arrays),
+        out_specs=(pl.BlockSpec(memory_space=pltpu.VMEM),) * len(arrays),
+        scratch_shapes=[pltpu.VMEM(a.shape, a.dtype) for a in arrays]
+        + [pltpu.SemaphoreType.DMA((len(arrays),))],
+        compiler_params=pltpu.CompilerParams(vmem_limit_bytes=62 * 1024 * 1024),
+        name="deliver",
+    )(*arrays)
 
 
 def shards(sizes, h, dy, pos, labels, entries, miller, kfilter, mix, table, radial):
@@ -527,30 +637,46 @@
         pltpu.VMEM((2 * k, ATOMS), bf16),
         pltpu.VMEM((plane, nc, 16, 128), f32),
         pltpu.VMEM((nx, nl, ny, nh, nc, 16, 128), bf16),
-        pltpu.VMEM((3, 3, 3, 16, 128), bf16),
-        pltpu.VMEM((5, 16, 128), bf16),
-        pltpu.VMEM((6, 3, 3, 16, 128), bf16),
-        pltpu.VMEM((12, 3, 16, 128), bf16),
-        pltpu.VMEM((8, 16, 128), bf16),
+        pltpu.VMEM((3, 3, 3, 8, 128), bf16),
+        pltpu.VMEM((5, 8, 128), bf16),
+        pltpu.VMEM((6, 3, 3, 8, 128), bf16),
+        pltpu.VMEM((12, 3, 8, 128), bf16),
+        pltpu.VMEM((8, 8, 128), bf16),
+        pltpu.VMEM((3, 3, 3, 1, 128), f32),
+        pltpu.VMEM((5, 1, 128), f32),
+    ]
+    for _ in range(3):
+        scratch += [
+            pltpu.VMEM((6, 3, 3, 1, 128), f32),
+            pltpu.VMEM((12, 3, 1, 128), f32),
+            pltpu.VMEM((8, 1, 128), f32),
+        ]
+    scratch += [
+        pltpu.VMEM((4 * CH, SEG), bf16),
+        pltpu.VMEM((BLOCKS, 128), f32),
+        pltpu.VMEM((NBR // GROUP, BLOCKS, GROUP * ATOMS), bf16),
+        pltpu.VMEM((96, GROUP * ATOMS), bf16),
+        pltpu.VMEM((BLOCKS, 96), f32),
+        pltpu.VMEM((32, 1, 128), f32),
         pltpu.VMEM((NBR, 8, ATOMS), i32),
-        pltpu.VMEM((NBR, SEG, ATOMS), bf16),
+        pltpu.VMEM((NBR // GROUP, SEG, GROUP * ATOMS), bf16),
         pltpu.VMEM((NBR, CH, ATOMS), bf16),
         pltpu.VMEM((NBR, CH, ATOMS), f32),
         pltpu.VMEM((NBR, NB, ATOMS), f32),
         pltpu.VMEM((NBR, 8, ATOMS), f32),
-        pltpu.VMEM((3 * FEAT, ATOMS), bf16),
+        pltpu.VMEM((4 * CH, GROUP * ATOMS), bf16),
         pltpu.VMEM((CH, ATOMS), f32),
-        pltpu.VMEM((SEG, 3 * FEAT), f32),
-        pltpu.VMEM((32, 16, 128), f32),
+        pltpu.VMEM((SEG, 4 * CH), f32),
+        pltpu.VMEM((32, 8, 128), f32),
         pltpu.VMEM((8, ATOMS), f32),
         pltpu.VMEM((CH, ATOMS), f32),
         pltpu.VMEM((2 * NB, 2 * CH), f32),
-        pltpu.VMEM((6, 3, 3, 16, 128), bf16),
-        pltpu.VMEM((12, 3, 16, 128), bf16),
-        pltpu.VMEM((8, 16, 128), bf16),
-        pltpu.VMEM((6, 3, 3, 16, 128), bf16),
-        pltpu.VMEM((12, 3, 16, 128), bf16),
-        pltpu.VMEM((8, 16, 128), bf16),
+        pltpu.VMEM((6, 3, 3, 8, 128), bf16),
+        pltpu.VMEM((12, 3, 8, 128), bf16),
+        pltpu.VMEM((8, 8, 128), bf16),
+        pltpu.VMEM((6, 3, 3, 8, 128), bf16),
+        pltpu.VMEM((12, 3, 8, 128), bf16),
+        pltpu.VMEM((8, 8, 128), bf16),
         pltpu.VMEM((plane, 16, 128), f32),
         pltpu.VMEM((nx, nl, ny, nh, 16, 128), bf16),
         pltpu.VMEM((nxy - 1, nl, nh, 16, 128), bf16),
@@ -564,9 +690,11 @@
         pltpu.VMEM((CH, ATOMS), f32),
         pltpu.VMEM((CH, ATOMS), f32),
         pltpu.VMEM((16, ATOMS), f32),
-        pltpu.VMEM((ROWS, CH), f32),
+        pltpu.VMEM((CH, 128), f32),
+        pltpu.VMEM((128, CH), f32),
         pltpu.VMEM((16, k), bf16),
         pltpu.VMEM((8, 128), f32),
+        pltpu.VMEM((3, ATOMS), f32),
         pltpu.VMEM((2, 24, 128), f32),
         pltpu.VMEM((24, 128), f32),
         pltpu.VMEM((nxy, 24, 128), f32),
@@ -574,13 +702,13 @@
         pltpu.VMEM((2, 24, 128), f32),
         dma,
     ]
-    for count in (26, 26, 1, nxy - 1, nz - 1, nz - 1, nxy - 1, 1, 1, nxy - 1, nz - 1, 1):
+    for count in (52, 52, 1, nxy - 1, nz - 1, nz - 1, nxy - 1, 1, 1, nxy - 1, nz - 1, 1):
         scratch += [dma((count,)), dma((count,))]
     out = pl.pallas_call(
         functools.partial(kernel, sizes),
         out_shape=(
             jax.ShapeDtypeStruct((CH, ATOMS), bf16),
-            jax.ShapeDtypeStruct((3, ATOMS), f32),
+            jax.ShapeDtypeStruct((3, 1, ATOMS), f32),
             jax.ShapeDtypeStruct((CH, CH), f32),
             jax.ShapeDtypeStruct((NB, CH), f32),
             jax.ShapeDtypeStruct((ROWS, CH), f32),
@@ -589,14 +717,15 @@
         out_specs=(vmem,) * 5,
         scratch_shapes=scratch,
         compiler_params=pltpu.CompilerParams(
-            collective_id=0, has_side_effects=True, vmem_limit_bytes=60 * 1024 * 1024
+            collective_id=0, has_side_effects=True, vmem_limit_bytes=62 * 1024 * 1024
         ),
         name="layer",
     )(
-        h[0, 0, 0], dy[0, 0, 0], pos[0, 0, 0], labels[0, 0], entries[0, 0, 0],
-        miller, kfilter, mix, table, radial,
+        h[0, 0, 0], dy[0, 0, 0], jnp.transpose(pos, (0, 1, 3, 2, 4))[0, 0], labels[0, 0], entries[0, 0, 0],
+        miller, kfilter.T, mix, table, radial,
     )
-    return (out[0][None, None, None], out[1][None, None, None], out[2], out[3], out[4])
+    out = deliver(out)
+    return (out[0][None, None, None], jnp.transpose(out[1][None, None], (0, 1, 3, 2, 4)), out[2], out[3], out[4])
 
 
 def solution(mesh):

time: 80.6 us -> 72.7 us (0.902)
  local copies, waits for them, and re-layouts: 8.39 us -> 0 us
    unnamed x17 -> x0, local copies, waits for them, and re-layouts: 8.39 us -> none
    pallas_call x0 -> x1, Pallas kernels: none -> 1.54 us  [deliver(): pl.pallas_call(deliver_kernel, out_shape=tuple((jax.ShapeDtypeStruct(a.sh...]
where the time goes in v2:
time: 72.7 us; the launch traced here: 72.6 us
  Pallas kernels  71.9 us (99%)
    pallas_call x1, Pallas kernels, shards(): pl.pallas_call(functools.partial(kernel, sizes), out_shape=(jax.ShapeDtyp...  70.4 us
    pallas_call x1, Pallas kernels, deliver(): pl.pallas_call(deliver_kernel, out_shape=tuple((jax.ShapeDtypeStruct(a.sh...  1.54 us

profile of v2, /device:TPU:1, one launch (start us, length us, event | category | flops | bytes accessed | tf_op | source)
XLA Modules:
  0.0 72.6 jit_solution(7844366819107383831)
XLA Ops:
  0.6 70.4 %layer.1 = (bf16[64,512]{1,0:T(8,128)(2,1)}, f32[3,1,512]{2,1,0:T(1,128)}, f32[64,64]{1,0:T(8,128)}, f32[16,64]{1,0:T(8,128)}, f32[8,64]{1,0:T(8,128)}) custom-call(bf16[64,512]{1,0:T(8,128)(2,1)} %bitcast.11, bf16[64,512]{1,0:T(8,128)(2,1)} %bitcast.12, f32[3,1,512]{2,1,0:T(1,128)} %bitcast.14, s32[1,512]{1,0:T(1,128)} %bitcast.15, s32[16,512]{1,0:T(8,128)} %bitcast.13, ...), custom_call_target="tpu_custom_call" | custom-call | tf_op jit(solution)/shard_map/layer/pallas_call | solution.py:707
  71.0 1.5 %deliver.1 = (bf16[64,512]{1,0:T(8,128)(2,1)}, f32[3,1,512]{2,1,0:T(1,128)}, f32[64,64]{1,0:T(8,128)}, f32[16,64]{1,0:T(8,128)}, f32[8,64]{1,0:T(8,128)}) custom-call(bf16[64,512]{1,0:T(8,128)(2,1)} %get-tuple-element.15.refs_0_, f32[3,1,512]{2,1,0:T(1,128)} %get-tuple-element.16.refs_1_, f32[64,64]{1,0:T(8,128)} %get-tuple-element.17.refs_2_, ...), custom_call_target="tpu_custom_call" | custom-call | tf_op jit(solution)/shard_map/deliver/pallas_call | solution.py:616

commit v3 on v2

--- a/solution.py
+++ b/solution.py
@@ -22,7 +22,8 @@
 ROWS = 8
 SEG = 528
 BLOCKS = 144
-GROUP = 4
+EWALD = 4
+GROUP = 8
 reach_sq = 0.75
 
 COS = (
@@ -102,7 +103,7 @@
 
 def kernel(
     sizes,
-    h_ref, dy_ref, pos_ref, lab_ref, idx_ref, mil_ref, kf_ref, mix_ref, gain_ref, rad_ref,
+    h_in, dy_in, pos_in, lab_in, idx_in, mil_in, kf_ref, mix_in, gain_in, rad_in,
     atom_out, pos_out, weight_out, radial_out, filter_out,
     cs, tot, arr,
     feat, feat5, gf, ge, gc,
@@ -112,6 +113,7 @@
     rec_a, a_bf, rec_b, sum_b, rec_c, g1,
     m9_s, p9_s, st_s, stt_s, gains_s, ew_s, ep_s, kf_s, kft_s, mi_s, tab_s, pos_s,
     ar_l, ar_r, ar_x, ar_z, ar_o,
+    h_ref, dy_ref, pos_ref, lab_ref, idx_ref, mil_ref, mix_ref, gain_ref, rad_ref, in_sem,
     kf_sem, gs, gr, bs, br, cs_s, cs_r, xs, xr, zs, zr, azs, azr, axs, axr, acs, acr,
     rcs, rcr, rxs, rxr, rzs, rzr, ros, ror,
 ):
@@ -156,6 +158,17 @@
         copy.start()
         return copy
 
+    in_copies = [
+        pltpu.make_async_copy(a, b, in_sem.at[n])
+        for n, (a, b) in enumerate(
+            (
+                (h_in, h_ref), (pos_in, pos_ref), (lab_in, lab_ref), (mix_in, mix_ref), (gain_in, gain_ref),
+                (mil_in, mil_ref), (dy_in, dy_ref), (idx_in, idx_ref), (rad_in, rad_ref),
+            )
+        )
+    ]
+    for c in in_copies:
+        c.start()
     kf_copy = pltpu.make_async_copy(kf_ref.at[:, pl.ds(pl.multiple_of(owner // 16 * 128, 128), 128)], kf_s, kf_sem)
     kf_copy.start()
 
@@ -163,6 +176,9 @@
     partners = [brick(*o) for o in GHOSTS] + [xy_dev(s) for s in xy_steps] + [z_dev(s) for s in z_steps] + [sibling]
     for dev in partners:
         pl.semaphore_signal(barrier, inc=1, device_id=dev, device_id_type=MESH)
+
+    for c in in_copies:
+        c.wait()
 
     hb = h_ref[...]
     tab_s[...] = jnp.zeros((8, 128), f32)
@@ -198,8 +214,10 @@
     stt_s[...] = jnp.transpose(st.astype(f32)).astype(bf16)
     mil = mil_ref[...].astype(f32)
     mrows = jnp.concatenate([mil, mil, mil, jnp.zeros((7, mil.shape[1]), f32)], axis=0)
-    mi_s[...] = mrows.astype(bf16)
-    m9_s[...] = jnp.transpose(mrows).astype(bf16)
+    mrows = jnp.transpose(mrows).reshape(devices // nc, nc, ROWS, 16)
+    mrows = jnp.concatenate([mrows[:, c] for c in range(nc)], axis=0).reshape(devices * ROWS, 16)
+    m9_s[...] = mrows.astype(bf16)
+    mi_s[...] = jnp.transpose(mrows).astype(bf16)
     absolute = jnp.concatenate(
         [
             (p[0:1] + x.astype(f32)) * (1.0 / nx),
@@ -213,7 +231,8 @@
     w_lo = (absolute - w_hi - w_mid).astype(bf16).astype(f32)
     p9_s[...] = jnp.concatenate([w_hi, w_mid, w_lo, jnp.zeros((7, ATOMS), f32)], axis=0).astype(bf16)
 
-    chunk = 16 if devices >= 16 else devices
+    chunk = 16
+    per_core = devices // nc // chunk
 
     def phase_step(n, _):
         at = pl.multiple_of(n * (chunk * ROWS), chunk * ROWS)
@@ -225,13 +244,13 @@
         both = jnp.concatenate([cosine, sine], axis=1).reshape(chunk * 2 * ROWS, ATOMS).astype(bf16)
         cs[pl.ds(pl.multiple_of(n * (chunk * 2 * ROWS), chunk * 2 * ROWS), chunk * 2 * ROWS), :] = both
         part = dot_nn(both, stt_s[...])
-        tot[pl.ds(n * (chunk // nc), chunk // nc)] = part.reshape(chunk // nc, nc, 16, 128)
+        tot[n // per_core, pl.ds(lax.rem(n, per_core) * chunk, chunk)] = part.reshape(chunk, 16, 128)
         return 0
 
     lax.fori_loop(0, devices // chunk, phase_step, 0)
 
     pl.semaphore_wait(barrier, len(partners))
-    core_copy = send(tot.at[:, nc - 1 - co], rec_a, cs_s.at[0], cs_r.at[0], sibling)
+    core_copy = send(tot.at[nc - 1 - co], rec_a, cs_s.at[0], cs_r.at[0], sibling)
 
     ghost_copies = [
         send(pick(feat, o), region(o, gf, ge, gc), gs.at[n], gr.at[n], brick(-o[0], -o[1], -o[2]))
@@ -272,7 +291,7 @@
     core_copy.wait_recv()
 
     def core_sum(n, _):
-        part = tot[pl.ds(n * (nl * ny * nh), nl * ny * nh), co] + rec_a[pl.ds(n * (nl * ny * nh), nl * ny * nh)]
+        part = tot[co, pl.ds(n * (nl * ny * nh), nl * ny * nh)] + rec_a[pl.ds(n * (nl * ny * nh), nl * ny * nh)]
         a_bf[n] = part.astype(bf16).reshape(nl, ny, nh, 16, 128)
         return 0
 
@@ -373,7 +392,22 @@
         agg_s[...] += functools.reduce(jnp.add, parts)
         return 0
 
-    lax.fori_loop(0, NBR // GROUP, forward_step, 0)
+    half = NBR // GROUP // 2
+    lax.fori_loop(0, half, forward_step, 0)
+
+    for c in xy_copies:
+        c.wait_recv()
+    part = a_bf[x, :, y].astype(f32)
+    for n in range(len(xy_steps)):
+        part = part + rec_b[n].astype(f32)
+    sum_b[...] = part
+
+    z_copies = []
+    for n, s in enumerate(z_steps):
+        th, tl = z_to(s)
+        z_copies.append(send(sum_b.at[tl, th], rec_c.at[n], zs.at[n], zr.at[n], z_dev(s)))
+
+    lax.fori_loop(half, NBR // GROUP, forward_step, 0)
 
     v = agg_s[...] * NBR ** (-0.5)
     sig = 1.0 / (1.0 + jnp.exp(-v))
@@ -417,20 +451,26 @@
         gradp_s[...] += dot_nt(hotb[n], dgp[...])
         return 0
 
-    half = NBR // GROUP // 2
     lax.fori_loop(0, half, backward_step, 0)
 
-    for c in xy_copies:
+    for c in z_copies:
         c.wait_recv()
-    part = a_bf[x, :, y].astype(f32)
-    for n in range(len(xy_steps)):
-        part = part + rec_b[n].astype(f32)
-    sum_b[...] = part
-
-    z_copies = []
-    for n, s in enumerate(z_steps):
-        th, tl = z_to(s)
-        z_copies.append(send(sum_b.at[tl, th], rec_c.at[n], zs.at[n], zr.at[n], z_dev(s)))
+    total = sum_b[zl, zh]
+    for n in range(len(z_steps)):
+        total = total + rec_c[n]
+    kf_copy.wait()
+    kft_s[...] = jnp.transpose(kf_s[...])
+    kf = kft_s[pl.ds(pl.multiple_of(lax.rem(owner, 16) * ROWS, ROWS), ROWS), :]
+    struct = total[:, 0:CH] * norm_atoms
+    back = total[:, CH : 2 * CH] * norm_k
+    prod = struct * back
+    filter_out[...] = prod[0:ROWS] + prod[ROWS : 2 * ROWS]
+    kf2 = jnp.concatenate([kf, kf], axis=0)
+    coeffs = jnp.concatenate([norm_atoms * kf2 * back, norm_k * kf2 * struct], axis=1).astype(bf16)
+    g1[zl, zh] = coeffs
+    az_copies = [
+        send(g1.at[zl, zh], g1.at[zl, zh], azs.at[n], azr.at[n], z_dev(s)) for n, s in enumerate(z_steps)
+    ]
 
     lax.fori_loop(half, NBR // GROUP, backward_step, 0)
 
@@ -454,65 +494,31 @@
         for n, o in enumerate(GHOSTS)
     ]
 
-    for c in z_copies:
-        c.wait_recv()
-    total = sum_b[zl, zh]
-    for n in range(len(z_steps)):
-        total = total + rec_c[n]
-    kf_copy.wait()
-    kft_s[...] = jnp.transpose(kf_s[...])
-    kf = kft_s[pl.ds(pl.multiple_of(lax.rem(owner, 16) * ROWS, ROWS), ROWS), :]
-    struct = total[:, 0:CH] * norm_atoms
-    back = total[:, CH : 2 * CH] * norm_k
-    prod = struct * back
-    filter_out[...] = prod[0:ROWS] + prod[ROWS : 2 * ROWS]
-    kf2 = jnp.concatenate([kf, kf], axis=0)
-    coeffs = jnp.concatenate([norm_atoms * kf2 * back, norm_k * kf2 * struct], axis=1).astype(bf16)
-    g1[zl, zh] = coeffs
-    az_copies = [
-        send(g1.at[zl, zh], g1.at[zl, zh], azs.at[n], azr.at[n], z_dev(s)) for n, s in enumerate(z_steps)
-    ]
-
     for c in az_copies:
         c.wait_recv()
-    arr[x, :, y, :, co] = g1[...]
+    arr[co, x, :, y] = g1[...]
     ax_copies = [
-        send(g1, arr.at[x, :, y, :, co], axs.at[n], axr.at[n], xy_dev(s)) for n, s in enumerate(xy_steps)
-    ]
-
-    for c in back_copies:
-        c.wait_recv()
+        send(g1, arr.at[co, x, :, y], axs.at[n], axr.at[n], xy_dev(s)) for n, s in enumerate(xy_steps)
+    ]
+
+    dr = drad_s[...]
+    dr = dr[0:NB, 0:CH] + (dr[NB : 2 * NB, 0:CH] + dr[0:NB, CH : 2 * CH]) + dr[NB : 2 * NB, CH : 2 * CH]
+
+    def blocks_of(o):
+        view = [range(3) if c == 0 else [1 - c] for c in o]
+        return [9 * i + 3 * k + l for i in view[0] for k in view[1] for l in view[2]]
+
+    for n, o in enumerate(GHOSTS):
+        back_copies[n].wait_recv()
     for o in GHOSTS:
-        got = region(o, rf, re, rc)[...].astype(f32)
-        view = [range(3) if c == 0 else [1 - c] for c in o]
-        got = got.reshape(-1, 8, 128)
-        gotp = region(o, prf, pre, prc)[...].reshape(-1, 1, 128)
-        n = 0
-        for i in view[0]:
-            for k in view[1]:
-                for l in view[2]:
-                    own_s[9 * i + 3 * k + l] += got[n]
-                    ownp_s[9 * i + 3 * k + l] += gotp[n]
-                    n += 1
+        got = region(o, rf, re, rc)[...].astype(f32).reshape(-1, 8, 128)
+        for n, b in enumerate(blocks_of(o)):
+            own_s[b] += got[n]
     own = own_s[...]
     own = jnp.concatenate([own[:, None, :, 0:CH], own[:, None, :, CH : 2 * CH]], axis=1)
     own = jnp.transpose(own.reshape(ATOMS, CH))
-    ownp = jnp.transpose(ownp_s[...].reshape(32, 128))[0:48]
-    wide = dot_nn(jnp.concatenate(split3(ownp), axis=1), jnp.concatenate([block_hot] * 3, axis=0))
-    ownp = jnp.concatenate(
-        [
-            jnp.sum(jnp.where(in_block, wide[16 * d : 16 * d + 16], 0.0), axis=0, keepdims=True)
-            for d in range(3)
-        ],
-        axis=0,
-    )
-    gains = gains_s[...]
-    zscaled = (own * gains).astype(bf16)
-    pos_short = ownp - ownpos_s[0:3]
-    ew_s[...] = dy_ref[...].astype(f32) + dot_nn(mix_ref[...], zscaled)
+    zscaled = (own * gains_s[...]).astype(bf16)
     weight = dot_nt(h_ref[...], zscaled)
-    dr = drad_s[...]
-    dr = dr[0:NB, 0:CH] + (dr[NB : 2 * NB, 0:CH] + dr[0:NB, CH : 2 * CH]) + dr[NB : 2 * NB, CH : 2 * CH]
     small = jnp.concatenate(
         [
             jnp.concatenate([weight[0:32], weight[32:64]], axis=1),
@@ -524,61 +530,79 @@
     ar_l[...] = small.reshape(2, 24, 128)
     rc_copy = send(ar_l.at[nc - 1 - co], ar_r, rcs.at[0], rcr.at[0], sibling)
 
+    for n, o in enumerate(GHOSTS):
+        back_copies[26 + n].wait_recv()
+    for o in GHOSTS:
+        got = region(o, prf, pre, prc)[...].reshape(-1, 1, 128)
+        for n, b in enumerate(blocks_of(o)):
+            ownp_s[b] += got[n]
     rc_copy.wait_recv()
-    ar_x[x * ny + y] = ar_l[co] + ar_r[...]
+    ar_x[x * ny + y] = (ar_l[co] + ar_r[...]).astype(bf16)
     rx_copies = [
         send(ar_x.at[x * ny + y], ar_x.at[x * ny + y], rxs.at[n], rxr.at[n], xy_dev(s))
         for n, s in enumerate(xy_steps)
     ]
+    ownp = jnp.transpose(ownp_s[...].reshape(32, 128))[0:48]
+    wide = dot_nn(jnp.concatenate(split3(ownp), axis=1), jnp.concatenate([block_hot] * 3, axis=0))
+    ownp = jnp.concatenate(
+        [
+            jnp.sum(jnp.where(in_block, wide[16 * d : 16 * d + 16], 0.0), axis=0, keepdims=True)
+            for d in range(3)
+        ],
+        axis=0,
+    )
+    pos_s[...] = ownp - ownpos_s[0:3]
+    ew_s[...] = dy_ref[...].astype(f32) + dot_nn(mix_ref[...], zscaled)
 
     for c in ax_copies:
         c.wait_recv()
-    ac_copy = send(
-        arr.at[:, :, :, :, co], arr.at[:, :, :, :, co], acs.at[0], acr.at[0], sibling
-    )
+    ac_copy = send(arr.at[co], arr.at[co], acs.at[0], acr.at[0], sibling)
+
+    ep_s[...] = jnp.zeros((16, ATOMS), f32)
+
+    per_x = per_core // nx
+
+    def ewald_one(step):
+        n = lax.rem(step + co * per_core, 2 * per_core)
+        rows_n = chunk * 2 * ROWS
+        m = lax.rem(n, per_core)
+        run = nl // per_x
+        co_n = arr[n // per_core, m // per_x, pl.ds(lax.rem(m, per_x) * run, run)].reshape(rows_n, 128)
+        cs_n = cs[pl.ds(pl.multiple_of(n * rows_n, rows_n), rows_n), :]
+        along = dot_nn(co_n, st_s[...]).reshape(chunk, 2, ROWS, ATOMS)
+        trig = cs_n.astype(f32).reshape(chunk, 2, ROWS, ATOMS)
+        ag = (along[:, 1] * trig[:, 0] - along[:, 0] * trig[:, 1]).reshape(chunk * ROWS, ATOMS)
+        m_n = mi_s[:, pl.ds(pl.multiple_of(n * (chunk * ROWS), chunk * ROWS), chunk * ROWS)]
+        co_t = jnp.transpose(co_n.astype(f32))[0:CH].astype(bf16)
+        return (
+            dot_nn(co_t, cs_n),
+            dot_nn(jnp.concatenate([m_n, m_n], axis=1), jnp.concatenate(split2(ag), axis=0)),
+        )
+
+    def ewald_step(step, _):
+        parts = [ewald_one(step * EWALD + k) for k in range(EWALD)]
+        ew_s[...] += functools.reduce(jnp.add, [p[0] for p in parts])
+        ep_s[...] += functools.reduce(jnp.add, [p[1] for p in parts])
+        return 0
+
+    steps = devices // chunk // EWALD
+    lax.fori_loop(0, steps // 2, ewald_step, 0)
     for c in rx_copies:
         c.wait_recv()
-    part = ar_x[0]
+    part = ar_x[0].astype(f32)
     for n in range(1, nx * ny):
-        part = part + ar_x[n]
+        part = part + ar_x[n].astype(f32)
     ar_z[zl * nh + zh] = part
     rz_copies = [
         send(ar_z.at[zl * nh + zh], ar_z.at[zl * nh + zh], rzs.at[n], rzr.at[n], z_dev(s))
         for n, s in enumerate(z_steps)
     ]
     ac_copy.wait_recv()
-
-    ep_s[...] = jnp.zeros((16, ATOMS), f32)
-
-    def ewald_step(n, _):
-        rows_n = chunk * 2 * ROWS
-        co_n = arr_chunk(n)
-        cs_n = cs[pl.ds(pl.multiple_of(n * rows_n, rows_n), rows_n), :]
-        along = dot_nn(co_n, st_s[...]).reshape(chunk, 2, ROWS, ATOMS)
-        trig = cs_n.astype(f32).reshape(chunk, 2, ROWS, ATOMS)
-        ag = (along[:, 1] * trig[:, 0] - along[:, 0] * trig[:, 1]).reshape(chunk * ROWS, ATOMS)
-        ag_hi, ag_lo = split2(ag)
-        m_n = mi_s[:, pl.ds(pl.multiple_of(n * (chunk * ROWS), chunk * ROWS), chunk * ROWS)]
-        ep_s[...] += dot_nn(m_n, ag_hi) + dot_nn(m_n, ag_lo)
-        co_t = jnp.transpose(co_n.astype(f32))[0:CH].astype(bf16)
-        ew_s[...] += dot_nn(co_t, cs_n)
-        return 0
-
-    per_x = nl * ny * nh * nc // chunk
-
-    def arr_chunk(n):
-        i = n // per_x
-        r = lax.rem(n, per_x)
-        if nl * ny * nh * nc // nl == chunk:
-            return arr[i, r].reshape(chunk * 16, 128)
-        return arr[i].reshape(chunk * 16, 128)
-
-    steps = devices // chunk
-    lax.fori_loop(0, steps, ewald_step, 0)
+    lax.fori_loop(steps // 2, steps, ewald_step, 0)
     atom_out[...] = ew_s[...].astype(bf16)
     ep = ep_s[0:3]
     turn = 2.0 * math.pi
-    pos_out[:, 0, :] = pos_short + jnp.concatenate(
+    pos_out[:, 0, :] = pos_s[...] + jnp.concatenate(
         [ep[0:1] * (turn / nx), ep[1:2] * (turn / n_gy), ep[2:3] * (turn / n_gz)], axis=0
     )
 
@@ -635,8 +659,8 @@
     plane = devices // nc
     scratch = [
         pltpu.VMEM((2 * k, ATOMS), bf16),
-        pltpu.VMEM((plane, nc, 16, 128), f32),
-        pltpu.VMEM((nx, nl, ny, nh, nc, 16, 128), bf16),
+        pltpu.VMEM((nc, plane, 16, 128), f32),
+        pltpu.VMEM((nc, nx, nl, ny, nh, 16, 128), bf16),
         pltpu.VMEM((3, 3, 3, 8, 128), bf16),
         pltpu.VMEM((5, 8, 128), bf16),
         pltpu.VMEM((6, 3, 3, 8, 128), bf16),
@@ -697,9 +721,19 @@
         pltpu.VMEM((3, ATOMS), f32),
         pltpu.VMEM((2, 24, 128), f32),
         pltpu.VMEM((24, 128), f32),
-        pltpu.VMEM((nxy, 24, 128), f32),
+        pltpu.VMEM((nxy, 24, 128), bf16),
         pltpu.VMEM((nz, 24, 128), f32),
         pltpu.VMEM((2, 24, 128), f32),
+        pltpu.VMEM((CH, ATOMS), bf16),
+        pltpu.VMEM((CH, ATOMS), bf16),
+        pltpu.VMEM((3, 1, ATOMS), f32),
+        pltpu.VMEM((1, ATOMS), i32),
+        pltpu.VMEM((NBR, ATOMS), i32),
+        pltpu.VMEM((3, k), i32),
+        pltpu.VMEM((CH, CH), bf16),
+        pltpu.VMEM((4, CH), f32),
+        pltpu.VMEM((NB, CH), f32),
+        dma((9,)),
         dma,
     ]
     for count in (52, 52, 1, nxy - 1, nz - 1, nz - 1, nxy - 1, 1, 1, nxy - 1, nz - 1, 1):
@@ -713,7 +747,7 @@
             jax.ShapeDtypeStruct((NB, CH), f32),
             jax.ShapeDtypeStruct((ROWS, CH), f32),
         ),
-        in_specs=[vmem] * 6 + [pl.BlockSpec(memory_space=pl.ANY)] + [vmem] * 3,
+        in_specs=[pl.BlockSpec(memory_space=pl.ANY)] * 10,
         out_specs=(vmem,) * 5,
         scratch_shapes=scratch,
         compiler_params=pltpu.CompilerParams(

time: 72.7 us -> 65.8 us (0.905)
  Pallas kernels: 71.9 us -> 64.8 us
    pallas_call x1, Pallas kernels: 70.4 us -> 63.3 us  [shards(): pl.pallas_call(functools.partial(kernel, sizes), out_shape=(jax.ShapeDtyp...]
where the time goes in v3:
time: 65.8 us; the launch traced here: 65.6 us
  Pallas kernels  64.8 us (98%)
  between operations  0.8 us (1%)
    pallas_call x1, Pallas kernels, shards(): pl.pallas_call(functools.partial(kernel, sizes), out_shape=(jax.ShapeDtyp...  63.3 us
    pallas_call x1, Pallas kernels, deliver(): pl.pallas_call(deliver_kernel, out_shape=tuple((jax.ShapeDtypeStruct(a.sh...  1.54 us

profile of v3, /device:TPU:1, one launch (start us, length us, event | category | flops | bytes accessed | tf_op | source)
XLA Modules:
  0.0 65.6 jit_solution(8069914437107043673)
XLA Ops:
  0.6 63.3 %layer.1 = (bf16[64,512]{1,0:T(8,128)(2,1)}, f32[3,1,512]{2,1,0:T(1,128)}, f32[64,64]{1,0:T(8,128)}, f32[16,64]{1,0:T(8,128)}, f32[8,64]{1,0:T(8,128)}) custom-call(bf16[64,512]{1,0:T(8,128)(2,1)} %bitcast.11, bf16[64,512]{1,0:T(8,128)(2,1)} %bitcast.12, f32[3,1,512]{2,1,0:T(1,128)} %bitcast.14, s32[1,512]{1,0:T(1,128)} %bitcast.15, s32[16,512]{1,0:T(8,128)} %bitcast.13, ...), custom_call_target="tpu_custom_call" | custom-call | tf_op jit(solution)/shard_map/layer/pallas_call | solution.py:741
  63.9 1.5 %deliver.1 = (bf16[64,512]{1,0:T(8,128)(2,1)}, f32[3,1,512]{2,1,0:T(1,128)}, f32[64,64]{1,0:T(8,128)}, f32[16,64]{1,0:T(8,128)}, f32[8,64]{1,0:T(8,128)}) custom-call(bf16[64,512]{1,0:T(8,128)(2,1)} %get-tuple-element.15.refs_0_, f32[3,1,512]{2,1,0:T(1,128)} %get-tuple-element.16.refs_1_, f32[64,64]{1,0:T(8,128)} %get-tuple-element.17.refs_2_, ...), custom_call_target="tpu_custom_call" | custom-call | tf_op jit(solution)/shard_map/deliver/pallas_call | solution.py:640

commit v4 on v3

--- a/solution.py
+++ b/solution.py
@@ -49,7 +49,7 @@
 FACES = [o for o in SLOTS if sum(map(abs, o)) == 1]
 EDGES = [o for o in SLOTS if sum(map(abs, o)) == 2]
 CORNERS = [o for o in SLOTS if sum(map(abs, o)) == 3]
-GHOSTS = FACES + EDGES + CORNERS
+GHOSTS = sorted(FACES + EDGES + CORNERS, key=lambda o: -abs(o[2]))
 
 
 def base_block(o):
@@ -626,14 +626,12 @@
 
 
 def deliver_kernel(*refs):
-    n = (len(refs) - 1) // 3
-    copies = [pltpu.make_async_copy(refs[i], refs[2 * n + i], refs[-1].at[i]) for i in range(n)]
+    n = (len(refs) - 1) // 2
+    copies = [pltpu.make_async_copy(refs[i], refs[n + i], refs[-1].at[i]) for i in range(n)]
     for c in copies:
         c.start()
     for c in copies:
         c.wait()
-    for i in range(n):
-        refs[n + i][...] = refs[2 * n + i][...]
 
 
 def deliver(arrays):
@@ -642,8 +640,7 @@
         out_shape=tuple(jax.ShapeDtypeStruct(a.shape, a.dtype) for a in arrays),
         in_specs=[pl.BlockSpec(memory_space=pl.ANY)] * len(arrays),
         out_specs=(pl.BlockSpec(memory_space=pltpu.VMEM),) * len(arrays),
-        scratch_shapes=[pltpu.VMEM(a.shape, a.dtype) for a in arrays]
-        + [pltpu.SemaphoreType.DMA((len(arrays),))],
+        scratch_shapes=[pltpu.SemaphoreType.DMA((len(arrays),))],
         compiler_params=pltpu.CompilerParams(vmem_limit_bytes=62 * 1024 * 1024),
         name="deliver",
     )(*arrays)

time: 65.8 us -> 65.7 us (level)
  no operation moved by 1% of the time
where the time goes in v4:
time: 65.7 us; the launch traced here: 65.5 us
  Pallas kernels  64.7 us (98%)
  between operations  0.8 us (1%)
    pallas_call x1, Pallas kernels, shards(): pl.pallas_call(functools.partial(kernel, sizes), out_shape=(jax.ShapeDtyp...  63.2 us
    pallas_call x1, Pallas kernels, deliver(): pl.pallas_call(deliver_kernel, out_shape=tuple((jax.ShapeDtypeStruct(a.sh...  1.54 us

profile of v4, /device:TPU:1, one launch (start us, length us, event | category | flops | bytes accessed | tf_op | source)
XLA Modules:
  0.0 65.5 jit_solution(17819424966838544035)
XLA Ops:
  0.6 63.2 %layer.1 = (bf16[64,512]{1,0:T(8,128)(2,1)}, f32[3,1,512]{2,1,0:T(1,128)}, f32[64,64]{1,0:T(8,128)}, f32[16,64]{1,0:T(8,128)}, f32[8,64]{1,0:T(8,128)}) custom-call(bf16[64,512]{1,0:T(8,128)(2,1)} %bitcast.11, bf16[64,512]{1,0:T(8,128)(2,1)} %bitcast.12, f32[3,1,512]{2,1,0:T(1,128)} %bitcast.14, s32[1,512]{1,0:T(1,128)} %bitcast.15, s32[16,512]{1,0:T(8,128)} %bitcast.13, ...), custom_call_target="tpu_custom_call" | custom-call | tf_op jit(solution)/shard_map/layer/pallas_call | solution.py:738
  63.8 1.5 %deliver.1 = (bf16[64,512]{1,0:T(8,128)(2,1)}, f32[3,1,512]{2,1,0:T(1,128)}, f32[64,64]{1,0:T(8,128)}, f32[16,64]{1,0:T(8,128)}, f32[8,64]{1,0:T(8,128)}) custom-call(bf16[64,512]{1,0:T(8,128)(2,1)} %get-tuple-element.15.refs_0_, f32[3,1,512]{2,1,0:T(1,128)} %get-tuple-element.16.refs_1_, f32[64,64]{1,0:T(8,128)} %get-tuple-element.17.refs_2_, ...), custom_call_target="tpu_custom_call" | custom-call | tf_op jit(solution)/shard_map/deliver/pallas_call | solution.py:638
